TPU v7x, 128 devices: a whole 4x4x4 slice. The times are simulated.
128 devices in a mesh: gx: 8 (over x, z_lo), gy: 16 (over z_hi, y, core).
Axes of the slice: x: 4, y: 4, z: 4 (z_hi: 2, z_lo: 2; z = z_hi * 2 + z_lo), core: 2. Of those that a mesh axis runs over, the one named last changes fastest.
Arguments:
- position: float32 [2, 48, 96, 128], P(None, 'gx', 'gy'), may hold values from 0 to 1
- velocity: float32 [2, 48, 96, 128], P(None, 'gx', 'gy'), may hold values from -3 to 3
- other_accel: float32 [2, 48, 96, 128], P(None, 'gx', 'gy'), may hold values from -5 to 5
- phase_ids: int32 [48, 96, 128], P('gx', 'gy'), may hold values from 0 to 1, as said below
- counts: int32 [48, 96], P('gx', 'gy'), may hold values from 48 to 128, as said below
Outputs:
- new_position: float32 [2, 48, 96, 128], P(None, 'gx', 'gy')
- new_velocity: float32 [2, 48, 96, 128], P(None, 'gx', 'gy')
- pressure: float32 [48, 96, 128], P('gx', 'gy')
- monitor: float32 [4, 4], replicated
Inputs may be any that keep to these rules, and one draw needn't show every extreme that they name: `counts`: each entry is the number of live slots of its cell; the live slots are the first ones of the cell; some cell holds 128. `phase_ids`: both phases occur among the live slots.
All inputs are finite; a program needn't handle non-finite values.
Results may differ from a plain program's by a relative error of at most 0.0001.
Values sent between devices are 32-bit elements; how exact they have to be, the bound alone decides.
A program may use at most 64 MiB of HBM per device.

v0:
```python
import jax
import jax.numpy as jnp
from jax import lax
from jax.sharding import Mesh
from jax.sharding import PartitionSpec as P

ITERS = 4
GX_GY = ("gx_0", "gx_1", "gy_0", "gy_1", "gy_2")
GX = ("gx_0", "gx_1")
GY = ("gy_0", "gy_1", "gy_2")


TIME_STEP = 0.05
KERNEL_NORM = 4.0 / (3.141592653589793 * 64.0)
REST_LIGHT = 1.2
REST_HEAVY = 1.5
STIFF_LIGHT = 100.0
STIFF_HEAVY = 200.0
MASS_LIGHT = 1.0
MASS_HEAVY = 1.5
SENTINEL = 1e30


def one_axis_at_a_time(value, axes):
    for axis in axes:
        value = lax.pmax(value, axis)
    return value


def padded(block, sides, width):
    for axis, dim in sides:
        count = lax.axis_size(axis)
        forward = [(i, i + 1) for i in range(count - 1)]
        forward.append((count - 1, 0))
        backward = [(target, source) for source, target in forward]
        low = lax.ppermute(
            lax.slice_in_dim(block, block.shape[dim] - width, None, axis=dim), axis, forward
        )
        high = lax.ppermute(lax.slice_in_dim(block, 0, width, axis=dim), axis, backward)
        block = jnp.concatenate([low, block, high], axis=dim)
    return block


def window_of(source, off_x, off_y, row_count, col_count):
    return source[1 + off_x : 1 + off_x + row_count, 1 + off_y : 1 + off_y + col_count]


def pair_sums(centers, padded_list, with_force):
    center_x, center_y = (centers[0], centers[1])
    near_x, near_y, near_live = (padded_list[0], padded_list[1], padded_list[2])
    row_count, col_count = (center_x.shape[0], center_x.shape[1])
    total_a = jnp.zeros_like(center_x)
    total_b = jnp.zeros_like(center_x)
    for off_x in (-1, 0, 1):
        for off_y in (-1, 0, 1):
            other_x = window_of(near_x, off_x, off_y, row_count, col_count)
            other_y = window_of(near_y, off_x, off_y, row_count, col_count)
            other_live = window_of(near_live, off_x, off_y, row_count, col_count)
            diff_x = center_x[..., :, None] - (other_x[..., None, :] + off_x)
            diff_y = center_y[..., :, None] - (other_y[..., None, :] + off_y)
            intersection = (
                jnp.maximum(1.0 - diff_x * diff_x - diff_y * diff_y, 0.0) * other_live[..., None, :]
            )
            if with_force:
                other_term = window_of(padded_list[3], off_x, off_y, row_count, col_count)
                pair_coef = (
                    intersection
                    * intersection
                    * (centers[2][..., :, None] + other_term[..., None, :])
                )
                total_a = total_a + jnp.sum(pair_coef * diff_x, axis=-1)
                total_b = total_b + jnp.sum(pair_coef * diff_y, axis=-1)
            else:
                total_a = total_a + jnp.sum(intersection * intersection * intersection, axis=-1)
    if with_force:
        return (total_a, total_b)
    return (total_a,)


def blocked(with_force, centers, padded_list, row_count):
    block_count = row_count // 2

    def one_block(block_index):
        first_row = block_index * 2
        center_part = tuple(
            (lax.dynamic_slice_in_dim(source, first_row, 2, 0) for source in centers)
        )
        padded_part = tuple(
            (lax.dynamic_slice_in_dim(source, first_row, 4, 0) for source in padded_list)
        )
        return pair_sums(center_part, padded_part, with_force)

    results = lax.map(one_block, jnp.arange(block_count, dtype=jnp.int32))
    return tuple((source.reshape((row_count,) + source.shape[2:]) for source in results))


def global_bounds(density_ratio, live_bool, heavy_bool):
    light_sel = live_bool & jnp.logical_not(heavy_bool)
    heavy_sel = live_bool & heavy_bool
    top_local = jnp.stack(
        [
            jnp.max(jnp.where(light_sel, density_ratio, -SENTINEL)),
            jnp.max(jnp.where(heavy_sel, density_ratio, -SENTINEL)),
        ]
    )
    low_local = jnp.stack(
        [
            jnp.min(jnp.where(light_sel, density_ratio, SENTINEL)),
            jnp.min(jnp.where(heavy_sel, density_ratio, SENTINEL)),
        ]
    )
    bounds = one_axis_at_a_time(jnp.concatenate([top_local, -low_local]), GX_GY)
    top_ratio = bounds[:2]
    low_ratio = -bounds[2:]
    return (top_ratio, low_ratio)


def phase_params(heavy_bool):
    rest_density = jnp.where(heavy_bool, REST_HEAVY, REST_LIGHT).astype(jnp.float32)
    stiffness = jnp.where(heavy_bool, STIFF_HEAVY, STIFF_LIGHT).astype(jnp.float32)
    return (rest_density, stiffness)


def pressure_update(pressure, density_sum, live_bool, heavy_bool, own_live, own_heavy, trim):
    live_mask = live_bool.astype(jnp.float32)
    rest_density, stiffness = phase_params(heavy_bool)
    density = KERNEL_NORM * density_sum
    density_ratio = density / rest_density
    own_ratio = density_ratio[
        trim : density_ratio.shape[0] - trim, trim : density_ratio.shape[1] - trim
    ]
    top_ratio, low_ratio = global_bounds(own_ratio, own_live, own_heavy)
    relaxation = 1.0 / (1.0 + top_ratio - low_ratio)
    particle_relax = jnp.where(heavy_bool, relaxation[1], relaxation[0])
    pressure = live_mask * (pressure + stiffness * particle_relax * (density_ratio - 1.0))
    safe_density = jnp.where(live_bool, density, 1.0)
    press_term = jnp.where(live_bool, pressure / (safe_density * safe_density), 0.0)
    return (pressure, press_term, jnp.concatenate([top_ratio, low_ratio]))


def local(position, velocity, other_accel, phase_ids, counts):
    tile_rows, tile_cols, slot_count = phase_ids.shape
    slot_index = jnp.arange(slot_count, dtype=jnp.int32)
    live_bool = slot_index[None, None, :] < counts[:, :, None]
    heavy_bool = phase_ids == 1
    live_mask = live_bool.astype(jnp.float32)
    particle_mass = jnp.where(heavy_bool, MASS_HEAVY, MASS_LIGHT).astype(jnp.float32)
    slot_codes = jnp.where(live_bool, phase_ids + 1, 0)
    padded_codes = padded(slot_codes, ((GX, 0), (GY, 1)), 2)
    cycle_codes = padded_codes[1:-1, 1:-1]
    cycle_live = cycle_codes > 0
    cycle_heavy = cycle_codes == 2
    cycle_mask = cycle_live.astype(jnp.float32)
    accel_x = jnp.zeros_like(live_mask)
    accel_y = jnp.zeros_like(live_mask)
    monitor_rows = []
    far_mask = (padded_codes > 0).astype(jnp.float32)
    cycle_pressure = jnp.zeros_like(cycle_mask)
    for iteration in range(ITERS):
        vel_x = velocity[0] + TIME_STEP * (other_accel[0] + accel_x)
        vel_y = velocity[1] + TIME_STEP * (other_accel[1] + accel_y)
        pos_x = position[0] + TIME_STEP * vel_x
        pos_y = position[1] + TIME_STEP * vel_y
        moved = padded(jnp.stack([pos_x, pos_y]), ((GX, 1), (GY, 2)), 2)
        cycle_x = moved[0, 1:-1, 1:-1]
        cycle_y = moved[1, 1:-1, 1:-1]
        (density_sum,) = blocked(
            False, (cycle_x, cycle_y), (moved[0], moved[1], far_mask), tile_rows + 2
        )
        cycle_pressure, cycle_term, monitor_row = pressure_update(
            cycle_pressure, density_sum, cycle_live, cycle_heavy, live_bool, heavy_bool, 1
        )
        force_x, force_y = blocked(
            True,
            (pos_x, pos_y, cycle_term[1:-1, 1:-1]),
            (cycle_x, cycle_y, cycle_mask, cycle_term),
            tile_rows,
        )
        accel_x = live_mask * (6.0 * KERNEL_NORM / particle_mass) * force_x
        accel_y = live_mask * (6.0 * KERNEL_NORM / particle_mass) * force_y
        monitor_rows.append(monitor_row)
    pressure = cycle_pressure[1:-1, 1:-1]
    new_vel_x = live_mask * (velocity[0] + TIME_STEP * (other_accel[0] + accel_x))
    new_vel_y = live_mask * (velocity[1] + TIME_STEP * (other_accel[1] + accel_y))
    new_pos_x = live_mask * (position[0] + TIME_STEP * new_vel_x)
    new_pos_y = live_mask * (position[1] + TIME_STEP * new_vel_y)
    return (
        jnp.stack([new_pos_x, new_pos_y]),
        jnp.stack([new_vel_x, new_vel_y]),
        pressure,
        jnp.stack(monitor_rows),
    )


def solution(mesh):
    torus = Mesh(mesh.devices.reshape(4, 2, 2, 4, 2), ("gx_0", "gx_1", "gy_0", "gy_1", "gy_2"))
    in_specs = (
        P(None, GX, GY, None),
        P(None, GX, GY, None),
        P(None, GX, GY, None),
        P(GX, GY, None),
        P(GX, GY),
    )
    out_specs = (P(None, GX, GY, None), P(None, GX, GY, None), P(GX, GY, None), P())
    return jax.shard_map(local, mesh=torus, in_specs=in_specs, out_specs=out_specs, check_vma=False)
```

profile of v0, /device:TPU:1, one launch (start us, length us, event | category | flops | bytes accessed | tf_op | source)
XLA Modules:
  0.0 439.0 jit_solution(13213212542423151397)
XLA Ops:
  7.3 3.6 collective-permute-start.1
  18.9 27.3 %while.88 = (s32[]{:T(128)}, f32[4,2,8,128]{3,2,1,0:T(8,128)S(1)}, s32[4]{0:T(128)S(1)}, f32[8,8,128]{2,1,0:T(8,128)S(1)}, f32[10,10,128]{2,1,0:T(8,128)S(1)}, /...) while((s32[]{:T(128)}, f32[4,2,8,128]{3,2,1,0:T(8,128)S(1)}, ...), condition=%wide.region_10.11_spmd, body=%wide.region_0.10_spmd.sunk | while | flops 25974796 | bytes 885060 | solution.py:93
  50.4 6.0 %pmax.140 = f32[4]{0:T(128)S(1)} all-reduce(f32[4]{0:T(128)S(1)} %pad_maximum_fusion.31), channel_id=1, replica_groups=mesh['gx_0'=4,'gx_1'=2,'gy_0'=2,'gy_1'=4,'gy_2'=2] {'gx_0'}, use_global_device_ids=true, to_apply=%region_15.16 | all-reduce | flops 4 | bytes 32 | tf_op jit(solution)/shard_map/pmax | solution.py:26
  56.4 6.1 %pmax.141 = f32[4]{0:T(128)S(1)} all-reduce(f32[4]{0:T(128)S(1)} %pmax.140), channel_id=1, replica_groups=mesh['gx_0'=4,'gx_1'=2,'gy_0'=2,'gy_1'=4,'gy_2'=2] {'gx_1'}, use_global_device_ids=true, to_apply=%region_16.17 | all-reduce | flops 4 | bytes 32 | tf_op jit(solution)/shard_map/pmax | solution.py:26
  62.6 6.1 %pmax.142 = f32[4]{0:T(128)S(1)} all-reduce(f32[4]{0:T(128)S(1)} %pmax.141), channel_id=1, replica_groups=mesh['gx_0'=4,'gx_1'=2,'gy_0'=2,'gy_1'=4,'gy_2'=2] {'gy_0'}, use_global_device_ids=true, to_apply=%region_17.18 | all-reduce | flops 4 | bytes 32 | tf_op jit(solution)/shard_map/pmax | solution.py:26
  68.7 14.8 %pmax.143 = f32[4]{0:T(128)S(1)} all-reduce(f32[4]{0:T(128)S(1)} %pmax.142), channel_id=1, replica_groups=mesh['gx_0'=4,'gx_1'=2,'gy_0'=2,'gy_1'=4,'gy_2'=2] {'gy_1'}, use_global_device_ids=true, to_apply=%region_18.19 | all-reduce | flops 4 | bytes 32 | tf_op jit(solution)/shard_map/pmax | solution.py:26
  88.1 26.8 %while.89 = (s32[]{:T(128)}, f32[3,2,6,128]{3,2,1,0:T(8,128)S(1)}, f32[3,2,6,128]{3,2,1,0:T(8,128)S(1)}, s32[3]{0:T(128)S(1)}, f32[6,6,128]{2,1,0:T(8,128)S(1)},...) while((s32[]{:T(128)}, f32[3,2,6,128]{3,2,1,0:T(8,128)S(1)}, ...), condition=%wide.region_39.40_spmd, body=%wide.region_20.39_spmd.sunk | while | flops 26557452 | bytes 1030516 | solution.py:93
  90.8 3.1 fusion.501
  93.9 3.1 fusion.500
  99.7 3.1 fusion.501
  102.8 3.1 fusion.500
  108.6 3.1 fusion.501
  111.8 3.1 fusion.500
  115.3 3.4 collective-permute-start.9
  119.8 3.0 collective-permute-start.10
  126.5 27.3 %while.90 = (s32[]{:T(128)}, f32[4,2,8,128]{3,2,1,0:T(8,128)S(1)}, s32[4]{0:T(128)S(1)}, f32[8,8,128]{2,1,0:T(8,128)S(1)}, f32[10,10,128]{2,1,0:T(8,128)S(1)}, /...) while((s32[]{:T(128)}, f32[4,2,8,128]{3,2,1,0:T(8,128)S(1)}, ...), condition=%wide.region_50.51_spmd, body=%wide.region_40.50_spmd.sunk | while | flops 25974796 | bytes 885060 | solution.py:93
  127.9 2.8 fusion.504
  134.7 2.8 fusion.504
  141.5 2.8 fusion.504
  148.3 2.8 fusion.504
  157.2 6.3 %pmax.145 = f32[4]{0:T(128)S(1)} all-reduce(f32[4]{0:T(128)S(1)} %pad_maximum_fusion.32), channel_id=1, replica_groups=mesh['gx_0'=4,'gx_1'=2,'gy_0'=2,'gy_1'=4,'gy_2'=2] {'gx_0'}, use_global_device_ids=true, to_apply=%region_55.56 | all-reduce | flops 4 | bytes 32 | tf_op jit(solution)/shard_map/pmax | solution.py:26
  163.5 6.1 %pmax.146 = f32[4]{0:T(128)S(1)} all-reduce(f32[4]{0:T(128)S(1)} %pmax.145), channel_id=1, replica_groups=mesh['gx_0'=4,'gx_1'=2,'gy_0'=2,'gy_1'=4,'gy_2'=2] {'gx_1'}, use_global_device_ids=true, to_apply=%region_56.57 | all-reduce | flops 4 | bytes 32 | tf_op jit(solution)/shard_map/pmax | solution.py:26
  169.6 5.6 %pmax.147 = f32[4]{0:T(128)S(1)} all-reduce(f32[4]{0:T(128)S(1)} %pmax.146), channel_id=1, replica_groups=mesh['gx_0'=4,'gx_1'=2,'gy_0'=2,'gy_1'=4,'gy_2'=2] {'gy_0'}, use_global_device_ids=true, to_apply=%region_57.58 | all-reduce | flops 4 | bytes 32 | tf_op jit(solution)/shard_map/pmax | solution.py:26
  175.2 12.3 %pmax.148 = f32[4]{0:T(128)S(1)} all-reduce(f32[4]{0:T(128)S(1)} %pmax.147), channel_id=1, replica_groups=mesh['gx_0'=4,'gx_1'=2,'gy_0'=2,'gy_1'=4,'gy_2'=2] {'gy_1'}, use_global_device_ids=true, to_apply=%region_58.59 | all-reduce | flops 4 | bytes 32 | tf_op jit(solution)/shard_map/pmax | solution.py:26
  187.5 3.2 pmax.149
  194.0 26.5 %while.91 = (s32[]{:T(128)}, f32[3,2,6,128]{3,2,1,0:T(8,128)S(1)}, f32[3,2,6,128]{3,2,1,0:T(8,128)S(1)}, s32[3]{0:T(128)S(1)}, f32[6,6,128]{2,1,0:T(8,128)S(1)},...) while((s32[]{:T(128)}, f32[3,2,6,128]{3,2,1,0:T(8,128)S(1)}, ...), condition=%wide.region_79.80_spmd, body=%wide.region_60.79_spmd.sunk | while | flops 26557452 | bytes 1030516 | solution.py:93
  196.6 3.1 fusion.508
  199.7 3.1 fusion.507
  205.4 3.1 fusion.508
  208.5 3.1 fusion.507
  214.3 3.1 fusion.508
  217.4 3.1 fusion.507
  225.5 3.3 collective-permute-start.14
  232.4 26.9 %while.92 = (s32[]{:T(128)}, f32[4,2,8,128]{3,2,1,0:T(8,128)S(1)}, s32[4]{0:T(128)S(1)}, f32[8,8,128]{2,1,0:T(8,128)S(1)}, f32[10,10,128]{2,1,0:T(8,128)S(1)}, /...) while((s32[]{:T(128)}, f32[4,2,8,128]{3,2,1,0:T(8,128)S(1)}, ...), condition=%wide.region_90.91_spmd, body=%wide.region_80.90_spmd.sunk | while | flops 25974796 | bytes 885060 | solution.py:93
  233.7 2.8 fusion.511
  253.9 2.8 fusion.511
  262.7 6.1 %pmax.150 = f32[4]{0:T(128)S(1)} all-reduce(f32[4]{0:T(128)S(1)} %pad_maximum_fusion.33), channel_id=1, replica_groups=mesh['gx_0'=4,'gx_1'=2,'gy_0'=2,'gy_1'=4,'gy_2'=2] {'gx_0'}, use_global_device_ids=true, to_apply=%region_95.96 | all-reduce | flops 4 | bytes 32 | tf_op jit(solution)/shard_map/pmax | solution.py:26
  268.8 6.1 %pmax.151 = f32[4]{0:T(128)S(1)} all-reduce(f32[4]{0:T(128)S(1)} %pmax.150), channel_id=1, replica_groups=mesh['gx_0'=4,'gx_1'=2,'gy_0'=2,'gy_1'=4,'gy_2'=2] {'gx_1'}, use_global_device_ids=true, to_apply=%region_96.97 | all-reduce | flops 4 | bytes 32 | tf_op jit(solution)/shard_map/pmax | solution.py:26
  274.9 5.4 %pmax.152 = f32[4]{0:T(128)S(1)} all-reduce(f32[4]{0:T(128)S(1)} %pmax.151), channel_id=1, replica_groups=mesh['gx_0'=4,'gx_1'=2,'gy_0'=2,'gy_1'=4,'gy_2'=2] {'gy_0'}, use_global_device_ids=true, to_apply=%region_97.98 | all-reduce | flops 4 | bytes 32 | tf_op jit(solution)/shard_map/pmax | solution.py:26
  280.3 12.3 %pmax.153 = f32[4]{0:T(128)S(1)} all-reduce(f32[4]{0:T(128)S(1)} %pmax.152), channel_id=1, replica_groups=mesh['gx_0'=4,'gx_1'=2,'gy_0'=2,'gy_1'=4,'gy_2'=2] {'gy_1'}, use_global_device_ids=true, to_apply=%region_98.99 | all-reduce | flops 4 | bytes 32 | tf_op jit(solution)/shard_map/pmax | solution.py:26
  292.6 3.4 pmax.154
  296.7 3.9 fusion.388
  300.6 27.0 %while.93 = (s32[]{:T(128)}, f32[3,2,6,128]{3,2,1,0:T(8,128)S(1)}, f32[3,2,6,128]{3,2,1,0:T(8,128)S(1)}, s32[3]{0:T(128)S(1)}, f32[6,6,128]{2,1,0:T(8,128)S(1)},...) while((s32[]{:T(128)}, f32[3,2,6,128]{3,2,1,0:T(8,128)S(1)}, ...), condition=%wide.region_119.120_spmd, body=%wide.region_100.119_spmd.sunk | while | flops 26557452 | bytes 1030516 | solution.py:93
  303.3 3.1 fusion.515
  306.4 3.1 fusion.514
  312.3 3.1 fusion.515
  315.4 3.1 fusion.514
  321.3 3.1 fusion.515
  324.4 3.1 fusion.514
  332.5 3.3 collective-permute-start.18
  339.4 27.5 %while.94 = (s32[]{:T(128)}, f32[4,2,8,128]{3,2,1,0:T(8,128)S(1)}, s32[4]{0:T(128)S(1)}, f32[8,8,128]{2,1,0:T(8,128)S(1)}, f32[10,10,128]{2,1,0:T(8,128)S(1)}, /...) while((s32[]{:T(128)}, f32[4,2,8,128]{3,2,1,0:T(8,128)S(1)}, ...), condition=%wide.region_130.131_spmd, body=%wide.region_120.130_spmd.sunk | while | flops 25974796 | bytes 885060 | solution.py:93
  370.2 6.1 %pmax.155 = f32[4]{0:T(128)S(1)} all-reduce(f32[4]{0:T(128)S(1)} %pad_maximum_fusion.34), channel_id=1, replica_groups=mesh['gx_0'=4,'gx_1'=2,'gy_0'=2,'gy_1'=4,'gy_2'=2] {'gx_0'}, use_global_device_ids=true, to_apply=%region_135.136 | all-reduce | flops 4 | bytes 32 | tf_op jit(solution)/shard_map/pmax | solution.py:26
  376.4 6.1 %pmax.156 = f32[4]{0:T(128)S(1)} all-reduce(f32[4]{0:T(128)S(1)} %pmax.155), channel_id=1, replica_groups=mesh['gx_0'=4,'gx_1'=2,'gy_0'=2,'gy_1'=4,'gy_2'=2] {'gx_1'}, use_global_device_ids=true, to_apply=%region_136.137 | all-reduce | flops 4 | bytes 32 | tf_op jit(solution)/shard_map/pmax | solution.py:26
  382.6 5.4 %pmax.157 = f32[4]{0:T(128)S(1)} all-reduce(f32[4]{0:T(128)S(1)} %pmax.156), channel_id=1, replica_groups=mesh['gx_0'=4,'gx_1'=2,'gy_0'=2,'gy_1'=4,'gy_2'=2] {'gy_0'}, use_global_device_ids=true, to_apply=%region_137.138 | all-reduce | flops 4 | bytes 32 | tf_op jit(solution)/shard_map/pmax | solution.py:26
  388.1 12.3 %pmax.158 = f32[4]{0:T(128)S(1)} all-reduce(f32[4]{0:T(128)S(1)} %pmax.157), channel_id=1, replica_groups=mesh['gx_0'=4,'gx_1'=2,'gy_0'=2,'gy_1'=4,'gy_2'=2] {'gy_1'}, use_global_device_ids=true, to_apply=%region_138.139 | all-reduce | flops 4 | bytes 32 | tf_op jit(solution)/shard_map/pmax | solution.py:26
  400.5 3.1 pmax.159
  404.3 5.1 %fusion.385 = (f32[8,8,128]{2,1,0:T(8,128)S(1)}, f32[8,8,128]{2,1,0:T(8,128)S(1)}) fusion(pred[8,8,128]{2,1,0:T(8,128)(4,1)S(1)} %get-tuple-element.763, f32[4,2,8,128]{3,2,1,0:T(8,128)S(1)} %broadcast_multiply_fusion, pred[8,8,128]{2,1,0:T(8,128)(4,1)S(1)} %get-tuple-element.768, f32[]{:T(128)} %bitcast.81, f32[]{:T(128)} %bitcast.80, ...), kind=kLoop, calls=%fused_computation.882 | loop fusion | flops 270336 | bytes 213024 | tf_op jit(solution)/shard_map/jit(_where)/select_n | solution.py:137
  409.5 26.8 %while.95 = (s32[]{:T(128)}, f32[3,2,6,128]{3,2,1,0:T(8,128)S(1)}, f32[3,2,6,128]{3,2,1,0:T(8,128)S(1)}, s32[3]{0:T(128)S(1)}, f32[6,6,128]{2,1,0:T(8,128)S(1)},...) while((s32[]{:T(128)}, f32[3,2,6,128]{3,2,1,0:T(8,128)S(1)}, ...), condition=%wide.region_159.160_spmd, body=%wide.region_140.159_spmd.sunk | while | flops 26557452 | bytes 1030516 | solution.py:93
  412.1 3.1 fusion.522
  415.3 3.1 fusion.521
  421.1 3.1 fusion.522
  424.2 3.1 fusion.521
  430.0 3.1 fusion.522
  433.1 3.1 fusion.521
  (347 shorter events, 167.6 us)
Async XLA Ops:
  0.6 5.7 %copy-start.2 = (f32[2,6,6,128]{3,0,2,1:T(2,128)S(1)}, f32[2,6,6,128]{3,0,2,1:T(2,128)}, u32[]{:S(2)}) copy-start(f32[2,6,6,128]{3,0,2,1:T(2,128)} %param.23) | copy-start | bytes 110596
  1.5 9.4 %collective-permute-start.4 = (s32[2,6,128]{2,1,0:T(8,128)S(1)}, s32[2,6,128]{2,1,0:T(8,128)S(1)}, u32[]{:S(2)}, u32[]{:S(2)}) collective-permute-start(s32[2,6,128]{2,1,0:T(8,128)S(1)} %get-tuple-element.1149), channel_id=1, source_target_pairs={{0,16},{16,32},{32,48},{48,64},{64,80},{80,96},{96,112},{112,0},{1... | collective-permute-start | bytes 18440 | tf_op jit(solution)/shard_map/ppermute | solution.py:36
  4.0 2.3 copy-start.3
  4.0 6.8 %collective-permute-start.5 = (s32[2,6,128]{2,1,0:T(8,128)S(1)}, s32[2,6,128]{2,1,0:T(8,128)S(1)}, u32[]{:S(2)}, u32[]{:S(2)}) collective-permute-start(s32[2,6,128]{2,1,0:T(8,128)S(1)} %get-tuple-element.1150), channel_id=1, source_target_pairs={{16,0},{32,16},{48,32},{64,48},{80,64},{96,80},{112,96},{0,112},{1... | collective-permute-start | bytes 18440 | tf_op jit(solution)/shard_map/ppermute | solution.py:39
  6.3 0.8 copy-start.4
  7.2 6.4 %collective-permute-start = (f32[2,2,6,128]{3,2,1,0:T(8,128)S(1)}, f32[2,2,6,128]{3,2,1,0:T(8,128)S(1)}, u32[]{:S(2)}, u32[]{:S(2)}) collective-permute-start(f32[2,2,6,128]{3,2,1,0:T(8,128)S(1)} %get-tuple-element.1139), channel_id=1, source_target_pairs={{0,16},{16,32},{32,48},{48,64},{64,80},{80,96},{96,112},{112,0},{1... | collective-permute-start | bytes 36872 | tf_op jit(solution)/shard_map/ppermute | solution.py:36
  7.3 6.4 %collective-permute-start.1 = (f32[2,2,6,128]{3,2,1,0:T(8,128)S(1)}, f32[2,2,6,128]{3,2,1,0:T(8,128)S(1)}, u32[]{:S(2)}, u32[]{:S(2)}) collective-permute-start(f32[2,2,6,128]{3,2,1,0:T(8,128)S(1)} %get-tuple-element.1140), channel_id=1, source_target_pairs={{16,0},{32,16},{48,32},{64,48},{80,64},{96,80},{112,96},{0,112},{1... | collective-permute-start | bytes 36872 | tf_op jit(solution)/shard_map/ppermute | solution.py:39
  10.8 7.1 %collective-permute-start.6 = (s32[10,2,128]{2,1,0:T(2,128)S(1)}, s32[10,2,128]{2,1,0:T(2,128)S(1)}, u32[]{:S(2)}, u32[]{:S(2)}) collective-permute-start(s32[10,2,128]{2,1,0:T(2,128)S(1)} %get-tuple-element.1141), channel_id=1, source_target_pairs={{0,1},{1,2},{2,3},{3,4},{4,5},{5,6},{6,7},{7,8},{8,9},{9,10},{10,1... | collective-permute-start | bytes 30728 | tf_op jit(solution)/shard_map/ppermute | solution.py:36
  13.6 4.4 collective-permute-start.7
  13.6 4.9 %collective-permute-start.2 = (f32[2,10,2,128]{3,2,1,0:T(2,128)S(1)}, f32[2,10,2,128]{3,2,1,0:T(2,128)S(1)}, u32[]{:S(2)}, u32[]{:S(2)}) collective-permute-start(f32[2,10,2,128]{3,2,1,0:T(2,128)S(1)} %get-tuple-element.1131), channel_id=1, source_target_pairs={{0,1},{1,2},{2,3},{3,4},{4,5},{5,6},{6,7},{7,8},{8,9},{9,10},{10,1... | collective-permute-start | bytes 61448 | tf_op jit(solution)/shard_map/ppermute | solution.py:36
  15.4 3.4 collective-permute-start.3
  46.3 0.7 copy-start
  46.3 0.7 copy-start.1
  115.0 4.8 %collective-permute-start.8 = (f32[2,2,6,128]{3,2,1,0:T(8,128)S(1)}, f32[2,2,6,128]{3,2,1,0:T(8,128)S(1)}, u32[]{:S(2)}, u32[]{:S(2)}) collective-permute-start(f32[2,2,6,128]{3,2,1,0:T(8,128)S(1)} %get-tuple-element.1137), channel_id=1, source_target_pairs={{0,16},{16,32},{32,48},{48,64},{64,80},{80,96},{96,112},{112,0},{1... | collective-permute-start | bytes 36872 | tf_op jit(solution)/shard_map/ppermute | solution.py:36
  115.3 4.5 %collective-permute-start.9 = (f32[2,2,6,128]{3,2,1,0:T(8,128)S(1)}, f32[2,2,6,128]{3,2,1,0:T(8,128)S(1)}, u32[]{:S(2)}, u32[]{:S(2)}) collective-permute-start(f32[2,2,6,128]{3,2,1,0:T(8,128)S(1)} %get-tuple-element.1138), channel_id=1, source_target_pairs={{16,0},{32,16},{48,32},{64,48},{80,64},{96,80},{112,96},{0,112},{1... | collective-permute-start | bytes 36872 | tf_op jit(solution)/shard_map/ppermute | solution.py:39
  119.8 3.9 collective-permute-start.10
  122.8 3.5 collective-permute-start.11
  220.7 4.8 %collective-permute-start.12 = (f32[2,2,6,128]{3,2,1,0:T(8,128)S(1)}, f32[2,2,6,128]{3,2,1,0:T(8,128)S(1)}, u32[]{:S(2)}, u32[]{:S(2)}) collective-permute-start(f32[2,2,6,128]{3,2,1,0:T(8,128)S(1)} %get-tuple-element.1135), channel_id=1, source_target_pairs={{0,16},{16,32},{32,48},{48,64},{64,80},{80,96},{96,112},{112,0},{1... | collective-permute-start | bytes 36872 | tf_op jit(solution)/shard_map/ppermute | solution.py:36
  222.5 2.9 collective-permute-start.13
  225.5 4.2 collective-permute-start.14
  228.8 3.5 collective-permute-start.15
  327.7 4.8 %collective-permute-start.16 = (f32[2,2,6,128]{3,2,1,0:T(8,128)S(1)}, f32[2,2,6,128]{3,2,1,0:T(8,128)S(1)}, u32[]{:S(2)}, u32[]{:S(2)}) collective-permute-start(f32[2,2,6,128]{3,2,1,0:T(8,128)S(1)} %get-tuple-element.1133), channel_id=1, source_target_pairs={{0,16},{16,32},{32,48},{48,64},{64,80},{80,96},{96,112},{112,0},{1... | collective-permute-start | bytes 36872 | tf_op jit(solution)/shard_map/ppermute | solution.py:36
  329.5 2.9 collective-permute-start.17
  332.5 4.2 collective-permute-start.18
  335.7 3.5 collective-permute-start.19
where the time goes:
time: 440 us; the launch traced here: 439 us
  other arithmetic  208 us (47%)
  blocking collectives  135 us (31%)
  starting transfers between devices  36 us (8%)
  local copies, waits for them, and re-layouts  24 us (5%)
  loops' own time  19.9 us (5%)
  waiting for transfers between devices  14.7 us (3%)
    pmax x20, blocking collectives, one_axis_at_a_time(): value = lax.pmax(value, axis)  135 us
    reduce_sum x36, other arithmetic, pair_sums(): total_b = total_b + jnp.sum(pair_coef * diff_y, axis=-1)  89.8 us
    reduce_sum x32, other arithmetic, pair_sums(): jnp.sum(intersection * intersection * intersection, axis=-1)  86.5 us
    ppermute x10, starting transfers between devices, padded(): lax.ppermute(lax.slice_in_dim(block, block.shape[dim] - width, None, axis...  20.6 us
    another operation x8, loops' own time, blocked(): results = lax.map(one_block, jnp.arange(block_count, dtype=jnp.int32))  19.9 us
    dynamic_slice x28, local copies, waits for them, and re-layouts, blocked(): results = lax.map(one_block, jnp.arange(block_count, dtype=jnp.int32))  16.9 us
    ppermute x10, starting transfers between devices, padded(): lax.ppermute(lax.slice_in_dim(block, 0, width, axis=dim), axis, backward)  15.4 us
    select_n x4, other arithmetic, pressure_update(): jnp.where(live_bool, pressure / (safe_density * safe_density), 0.0)  13 us
  transfers between devices with their start and end apart: 20, of which 11 were waited for; matrix products, arithmetic and copies ran while one was open for 0% of the time, Pallas kernels for 0%

commit v1 on v0

v1 whole, which is shorter than its diff:
```python
import functools

import jax
import jax.numpy as jnp
from jax import lax
from jax.experimental import pallas as pl
from jax.experimental.pallas import tpu as pltpu
from jax.sharding import PartitionSpec as P

ITERS = 4
TIME_STEP = 0.05
KERNEL_NORM = 4.0 / (3.141592653589793 * 64.0)
REST_LIGHT = 1.2
REST_HEAVY = 1.5
STIFF_LIGHT = 100.0
STIFF_HEAVY = 200.0
MASS_LIGHT = 1.0
MASS_HEAVY = 1.5
FAR = float(2**30)
NEG = -1e30
MESH = pl.DeviceIdType.MESH
ROWS = 6
COLS = 6
FS = 64
DIRS = ((-1, 0), (1, 0), (0, -1), (0, 1), (-1, -1), (-1, 1), (1, -1), (1, 1))

f32 = jnp.float32
bf16 = jnp.bfloat16


def rnd(v):
    return v.astype(bf16).astype(f32)


def split3(v):
    h = rnd(v)
    r = v - h
    m = rnd(r)
    return h, m, rnd(r - m)


def kernel(
    pos_ref, vel_ref, oa_ref, code_ref,
    npos_ref, nvel_ref, pres_ref, mon_ref,
    st, xp, tp, stage, tstage, rb, trb, fb, ib, lt, wb, dens, tf, mb, al, be, ar0, ar1, ar2,
    hs, hr, ts, tr, a1s, a1r, a2s, a2r,
):
    gx = lax.axis_index("gx")
    gy = lax.axis_index("gy")
    nx = lax.axis_size("gx")
    ny = lax.axis_size("gy")

    def around(dx, dy):
        return (lax.rem(gx + dx + nx, nx), lax.rem(gy + dy + ny, ny))

    barrier = pltpu.get_barrier_semaphore()
    partners = []
    for dx, dy in DIRS:
        partners.append(around(dx, dy))
    for d in range(2, ny - 1):
        partners.append(around(0, d))
    for d in range(2, nx - 1):
        partners.append(around(d, 0))
    for partner in partners:
        pl.semaphore_signal(barrier, inc=1, device_id=partner, device_id_type=MESH)

    st[...] = jnp.zeros_like(st)
    dens[...] = jnp.zeros_like(dens)
    mb[...] = jnp.zeros_like(mb)
    for a in range(ROWS):
        for f in range(2):
            st[f, a, 0:COLS, :] = pos_ref[f, a]
            st[2 + f, a, 0:COLS, :] = vel_ref[f, a]
            st[9 + f, a, 0:COLS, :] = oa_ref[f, a]
        code = code_ref[a]
        st[4, a, 0:COLS, :] = (code > 0.5).astype(f32)
        st[5, a, 0:COLS, :] = (code > 1.5).astype(f32)

    k = lax.broadcasted_iota(jnp.int32, (16, 128), 0)
    for ox in (-1, 0, 1):
        for oy in (-1, 0, 1):
            o = (ox + 1) * 3 + oy + 1
            al[o] = jnp.where(
                k < 2, 1.0,
                jnp.where((k >= 8) & (k < 11), 2.0 * ox, jnp.where((k >= 11) & (k < 14), 2.0 * oy, 0.0)),
            )
            be[o] = jnp.where(
                (k >= 2) & (k < 5), -2.0 * ox,
                jnp.where(
                    (k >= 5) & (k < 8), -2.0 * oy, jnp.where(k == 14, 1.0 - ox * ox - oy * oy, 0.0)
                ),
            )

    sub = lax.broadcasted_iota(jnp.int32, (8, 128), 0)
    col_at = jnp.where(sub == 7, -1, sub).astype(f32) - 2.5
    lane = lax.broadcasted_iota(jnp.int32, (1, 128), 1)

    pl.semaphore_wait(barrier, len(partners))

    def halo_copies(it, src, staged, dst, send, recv):
        copies = []
        for d, (dx, dy) in enumerate(DIRS):
            if d == 0:
                source = src.at[:, 1]
            elif d == 1:
                source = src.at[:, ROWS]
            else:
                source = staged.at[d]
            copies.append(
                pltpu.make_async_remote_copy(
                    src_ref=source,
                    dst_ref=dst.at[it, d],
                    send_sem=send.at[it, d],
                    recv_sem=recv.at[it, d],
                    device_id=around(dx, dy),
                    device_id_type=MESH,
                )
            )
        return copies

    def pack(src, staged, fields):
        for f in range(fields):
            for a in range(ROWS):
                staged[2, f, a, :] = src[f, a + 1, 0, :]
                staged[3, f, a, :] = src[f, a + 1, COLS - 1, :]
            staged[4, f, 0, :] = src[f, 1, 0, :]
            staged[5, f, 0, :] = src[f, 1, COLS - 1, :]
            staged[6, f, 0, :] = src[f, ROWS, 0, :]
            staged[7, f, 0, :] = src[f, ROWS, COLS - 1, :]

    def unpack(it, dst, got, fields):
        for f in range(fields):
            dst[f, ROWS + 1] = got[it, 0, f]
            dst[f, 0] = got[it, 1, f]
            for a in range(ROWS):
                dst[f, a + 1, 6, :] = got[it, 2, f, a, :]
                dst[f, a + 1, 7, :] = got[it, 3, f, a, :]
            dst[f, ROWS + 1, 6, :] = got[it, 4, f, 0, :]
            dst[f, ROWS + 1, 7, :] = got[it, 5, f, 0, :]
            dst[f, 0, 6, :] = got[it, 6, f, 0, :]
            dst[f, 0, 7, :] = got[it, 7, f, 0, :]

    def put(buf, index, value):
        for r in range(value.shape[0]):
            buf[index * FS + r * 8 : index * FS + r * 8 + 8, :] = value[r]

    def put_own(buf, index, value):
        for r in range(value.shape[0]):
            buf[index * FS + r * 8 + 8 : index * FS + r * 8 + 16, :] = value[r]

    def iteration(it, carry):
        live = st[4]
        heavy = st[5]
        alive = live > 0.5
        for f in range(2):
            v = st[2 + f] + TIME_STEP * (st[9 + f] + st[7 + f])
            x = st[f] + TIME_STEP * v - 0.5
            xp[f, 1 : ROWS + 1] = jnp.where(alive, x, FAR)
        pack(xp, stage, 2)
        copies = halo_copies(it, xp, stage, rb, hs, hr)
        for copy in copies:
            copy.start()
        for copy in copies:
            copy.wait()
        unpack(it, xp, rb, 2)

        x = xp[0]
        y = xp[1]
        xs = split3(x)
        ys = split3(y)
        rs = split3(x * x + y * y)
        one = jnp.ones_like(x)
        zero = jnp.zeros_like(x)
        h, m, l = 0, 1, 2
        jrow = (
            [xs[q] for q in (h, h, m, m, l, h)] + [ys[q] for q in (h, h, m, m, l, h)]
            + list(rs) + [one, one, one] + list(xs) + list(ys) + [one] * 7 + [zero]
        )
        irow = (
            [2.0 * xs[q] for q in (h, m, h, m, h, l)] + [2.0 * ys[q] for q in (h, m, h, m, h, l)]
            + [-one] * 3 + [-q for q in rs] + [zero] * 6 + list(xs) + list(ys) + [zero, zero]
        )
        for q in range(32):
            put(fb, q, jrow[q])
            put_own(ib, q, irow[q][1 : ROWS + 1])

        def transposes(r, c):
            for g in range(3):
                parts = []
                for b in range(2 * g - 1, 2 * g + 3):
                    parts.append(fb[pl.ds(r * 8 + b % 8, 32, stride=FS), :])
                lt[r * 3 + g] = jnp.concatenate(parts, axis=0).T.astype(bf16)
            return c

        lax.fori_loop(0, ROWS + 2, transposes, 0)

        def density(a, c):
            for g in range(3):
                base = []
                for e in range(2):
                    base.append(ib[pl.ds((a + 1) * 8 + 2 * g + e, 32, stride=FS), :])
                total = jnp.zeros((8, 256), f32)
                for ox in (-1, 0, 1):
                    left = lt[(a + 1 + ox) * 3 + g]
                    for n in range(3):
                        o = (ox + 1) * 3 + n
                        halves = []
                        for e in range(2):
                            part = jnp.concatenate(
                                [base[e][0:16], base[e][16:32] * al[o] + be[o]], axis=0
                            ).astype(bf16)
                            pieces = []
                            if n + e > 0:
                                pieces.append(jnp.zeros((32 * (n + e), 128), bf16))
                            pieces.append(part)
                            if n + e < 3:
                                pieces.append(jnp.zeros((32 * (3 - n - e), 128), bf16))
                            halves.append(jnp.concatenate(pieces, axis=0))
                        right = jnp.concatenate(halves, axis=1)
                        w = jnp.maximum(jnp.dot(left, right, preferred_element_type=f32), 0.0)
                        w2 = w * w
                        wb[(a * 3 + g) * 9 + o] = w2
                        total = total + jnp.sum((w2 * w).reshape(16, 8, 256), axis=0)
                row = jnp.sum(total, axis=0, keepdims=True)
                dens[a, 2 * g : 2 * g + 1, :] = row[:, 0:128]
                dens[a, 2 * g + 1 : 2 * g + 2, :] = row[:, 128:256]
            return c

        lax.fori_loop(0, ROWS, density, 0)

        density_now = KERNEL_NORM * dens[...]
        hot = heavy > 0.5
        ratio = density_now / jnp.where(hot, REST_HEAVY, REST_LIGHT)
        lit = alive & jnp.logical_not(hot)
        hvy = alive & hot
        peaks = (
            jnp.where(lit, ratio, NEG), jnp.where(hvy, ratio, NEG),
            jnp.where(lit, -ratio, NEG), jnp.where(hvy, -ratio, NEG),
        )
        vec = jnp.full((1, 128), NEG, f32)
        for q in range(4):
            top = jnp.max(jnp.max(peaks[q], axis=0), axis=0, keepdims=True)
            top = jnp.max(top, axis=1, keepdims=True)
            vec = jnp.where(lane == q, top, vec)

        ar0[it, 0] = vec
        first = []
        for d in range(1, ny):
            first.append(
                pltpu.make_async_remote_copy(
                    src_ref=ar0.at[it, 0], dst_ref=ar1.at[it, d],
                    send_sem=a1s.at[it, d], recv_sem=a1r.at[it, d],
                    device_id=around(0, d), device_id_type=MESH,
                )
            )
        for copy in first:
            copy.start()

        safe = jnp.where(alive, density_now, 1.0)
        inverse = 1.0 / (safe * safe)
        excess = jnp.where(hot, STIFF_HEAVY, STIFF_LIGHT) * (ratio - 1.0)
        t0 = jnp.where(alive, st[6] * inverse, 0.0)
        u = excess * inverse
        u0 = jnp.where(lit, u, 0.0)
        u1 = jnp.where(hvy, u, 0.0)
        tp[0, 1 : ROWS + 1] = t0
        tp[1, 1 : ROWS + 1] = u0
        tp[2, 1 : ROWS + 1] = u1
        pack(tp, tstage, 3)
        tcopies = halo_copies(it, tp, tstage, trb, ts, tr)
        for copy in tcopies:
            copy.start()
        for copy in tcopies:
            copy.wait()
        unpack(it, tp, trb, 3)

        for copy in first:
            copy.wait()
        best = vec
        for d in range(1, ny):
            best = jnp.maximum(best, ar1[it, d])
        ar0[it, 1] = best
        second = []
        for d in range(1, nx):
            second.append(
                pltpu.make_async_remote_copy(
                    src_ref=ar0.at[it, 1], dst_ref=ar2.at[it, d],
                    send_sem=a2s.at[it, d], recv_sem=a2r.at[it, d],
                    device_id=around(d, 0), device_id_type=MESH,
                )
            )
        for copy in second:
            copy.start()

        def moments(r, c):
            shift = lax.convert_element_type(r, f32) - 3.5
            px = xp[0, r] + shift
            py = xp[1, r] + col_at
            fields = (None, tp[0, r], tp[1, r], tp[2, r])
            base = r * 8
            if True:
                for q in range(4):
                    for e, p in enumerate((px, py)):
                        value = p if fields[q] is None else p * fields[q]
                        for level, piece in enumerate(split3(value)):
                            fb[pl.ds((level * 8 + 2 * q + e) * FS + base, 8), :] = piece
                    if fields[q] is None:
                        hi, lo = jnp.ones_like(px), jnp.zeros_like(px)
                    else:
                        hi = rnd(fields[q])
                        lo = rnd(fields[q] - hi)
                    fb[pl.ds((24 + q) * FS + base, 8), :] = hi
                    fb[pl.ds((28 + q) * FS + base, 8), :] = lo
            for b in range(-1, COLS + 1):
                tf[r, b + 1] = fb[pl.ds(base + b % 8, 32, stride=FS), :].astype(bf16)
            return c

        lax.fori_loop(0, ROWS + 2, moments, 0)

        def force(a, c):
            for g in range(3):
                total = jnp.zeros((64, 256), f32)
                for ox in (-1, 0, 1):
                    for n in range(3):
                        o = (ox + 1) * 3 + n
                        w2 = wb[(a * 3 + g) * 9 + o]
                        hi = w2.astype(bf16)
                        lo = (w2 - hi.astype(f32)).astype(bf16)
                        left = tf[a + 1 + ox, 2 * g + n : 2 * g + n + 2].reshape(64, 128)
                        both = jnp.concatenate([left, left], axis=1)
                        total = total + jnp.dot(
                            both, jnp.concatenate([hi, lo], axis=0), preferred_element_type=f32
                        )
                for e in range(2):
                    part = total[32 * e : 32 * e + 32, 128 * e : 128 * e + 128]
                    row = a * 8 + 2 * g + e
                    mb[pl.ds(row, 8, stride=FS), :] = part[0:8] + part[8:16] + part[16:24]
                    mb[pl.ds(8 * FS + row, 8, stride=FS), :] = part[24:32]
            return c

        lax.fori_loop(0, ROWS, force, 0)

        for copy in second:
            copy.wait()
        for d in range(1, nx):
            best = jnp.maximum(best, ar2[it, d])
        mon_ref[pl.ds(it, 1), :] = jnp.where(lane < 2, best, -best)[:, 0:4]
        relax0 = 1.0 / (1.0 + best[:, 0:1] + best[:, 2:3])
        relax1 = 1.0 / (1.0 + best[:, 1:2] + best[:, 3:4])
        relax0 = jnp.broadcast_to(relax0, (8, 128))
        relax1 = jnp.broadcast_to(relax1, (8, 128))

        for a in range(ROWS):
            def mom(q):
                return mb[q * FS + a * 8 : q * FS + a * 8 + 8, :]

            on = alive[a]
            ti = t0[a] + relax0 * u0[a] + relax1 * u1[a]
            s1 = mom(8) + mom(12)
            s_t = (mom(9) + mom(13)) + relax0 * (mom(10) + mom(14)) + relax1 * (mom(11) + mom(15))
            factor = 6.0 * KERNEL_NORM / jnp.where(hot[a], MASS_HEAVY, MASS_LIGHT)
            for f in range(2):
                p = xp[f, a + 1] + (a - 2.5 if f == 0 else col_at)
                s_p = mom(f)
                s_tp = mom(2 + f) + relax0 * mom(4 + f) + relax1 * mom(6 + f)
                push = ti * (p * s1 - s_p) + p * s_t - s_tp
                st[7 + f, a] = jnp.where(on, factor * push, 0.0)
            relax = jnp.where(hot[a], relax1, relax0)
            st[6, a] = jnp.where(on, st[6, a] + relax * excess[a], 0.0)
        return carry

    lax.fori_loop(0, ITERS, iteration, 0)

    live = st[4]
    for f in range(2):
        v = live * (st[2 + f] + TIME_STEP * (st[9 + f] + st[7 + f]))
        p = live * (st[f] + TIME_STEP * v)
        for a in range(ROWS):
            nvel_ref[f, a] = v[a, 0:COLS]
            npos_ref[f, a] = p[a, 0:COLS]
    for a in range(ROWS):
        pres_ref[a] = st[6, a, 0:COLS, :]


def local(nx, ny, position, velocity, other_accel, phase_ids, counts):
    slot = jnp.arange(128, dtype=jnp.int32)
    code = jnp.where(slot[None, None, :] < counts[:, :, None], phase_ids + 1, 0).astype(f32)
    vmem = pl.BlockSpec(memory_space=pltpu.VMEM)
    dma = pltpu.SemaphoreType.DMA
    return pl.pallas_call(
        kernel,
        out_shape=(
            jax.ShapeDtypeStruct((2, ROWS, COLS, 128), f32),
            jax.ShapeDtypeStruct((2, ROWS, COLS, 128), f32),
            jax.ShapeDtypeStruct((ROWS, COLS, 128), f32),
            jax.ShapeDtypeStruct((ITERS, 4), f32),
        ),
        in_specs=[vmem] * 4,
        out_specs=[vmem] * 4,
        scratch_shapes=[
            pltpu.VMEM((11, ROWS, 8, 128), f32),
            pltpu.VMEM((2, 8, 8, 128), f32),
            pltpu.VMEM((3, 8, 8, 128), f32),
            pltpu.VMEM((8, 2, 8, 128), f32),
            pltpu.VMEM((8, 3, 8, 128), f32),
            pltpu.VMEM((ITERS, 8, 2, 8, 128), f32),
            pltpu.VMEM((ITERS, 8, 3, 8, 128), f32),
            pltpu.VMEM((32 * FS, 128), f32),
            pltpu.VMEM((32 * FS, 128), f32),
            pltpu.VMEM((24, 128, 128), bf16),
            pltpu.VMEM((162, 128, 256), f32),
            pltpu.VMEM((ROWS, 8, 128), f32),
            pltpu.VMEM((8, 8, 32, 128), bf16),
            pltpu.VMEM((16 * FS, 128), f32),
            pltpu.VMEM((9, 16, 128), f32),
            pltpu.VMEM((9, 16, 128), f32),
            pltpu.VMEM((ITERS, 2, 1, 128), f32),
            pltpu.VMEM((ITERS, ny, 1, 128), f32),
            pltpu.VMEM((ITERS, nx, 1, 128), f32),
            dma((ITERS, 8)), dma((ITERS, 8)), dma((ITERS, 8)), dma((ITERS, 8)),
            dma((ITERS, ny)), dma((ITERS, ny)), dma((ITERS, nx)), dma((ITERS, nx)),
        ],
        compiler_params=pltpu.CompilerParams(
            collective_id=0, has_side_effects=True, vmem_limit_bytes=60 * 1024 * 1024
        ),
    )(position, velocity, other_accel, code)


def solution(mesh):
    in_specs = (
        P(None, "gx", "gy", None),
        P(None, "gx", "gy", None),
        P(None, "gx", "gy", None),
        P("gx", "gy", None),
        P("gx", "gy"),
    )
    out_specs = (P(None, "gx", "gy", None), P(None, "gx", "gy", None), P("gx", "gy", None), P())
    run = functools.partial(local, mesh.shape["gx"], mesh.shape["gy"])
    return jax.shard_map(run, mesh=mesh, in_specs=in_specs, out_specs=out_specs, check_vma=False)
```

time: 440 us -> 108 us (0.25)
  other arithmetic: 208 us -> 1.43 us
  blocking collectives: 135 us -> 0 us
  Pallas kernels: 0 us -> 98.6 us
  starting transfers between devices: 36 us -> 0 us
  loops' own time: 19.9 us -> 0 us
  local copies, waits for them, and re-layouts: 24 us -> 5.59 us
  waiting for transfers between devices: 14.7 us -> 0 us
    reduce_sum x68 -> x0, other arithmetic: 176 us -> none  [the longest x36 89.8 us: pair_sums(): total_b = total_b + jnp.sum(pair_coef * diff_y, axis=-1)]
    pmax x20 -> x0, blocking collectives: 135 us -> none  [one_axis_at_a_time(): value = lax.pmax(value, axis)]
    pallas_call x0 -> x1, Pallas kernels: none -> 98.6 us  [local(): pl.pallas_call(kernel, out_shape=(jax.ShapeDtypeStruct((2, ROWS, COLS, 12...]
    ppermute x20 -> x0, starting transfers between devices: 36 us -> none  [the longest x10 20.6 us: padded(): lax.ppermute(lax.slice_in_dim(block, block.shape[dim] - width, None, axis...]
    another operation x8 -> x0, loops' own time: 19.9 us -> none  [blocked(): results = lax.map(one_block, jnp.arange(block_count, dtype=jnp.int32))]
    dynamic_slice x56 -> x0, local copies, waits for them, and re-layouts: 17.1 us -> none  [the longest x28 16.9 us: blocked(): results = lax.map(one_block, jnp.arange(block_count, dtype=jnp.int32))]
    ppermute x20 -> x0, waiting for transfers between devices: 14.7 us -> none  [the longest x10 8.04 us: padded(): lax.ppermute(lax.slice_in_dim(block, 0, width, axis=dim), axis, backward)]
    select_n x5 -> x0, other arithmetic: 13.8 us -> none  [the longest x4 13 us: pressure_update(): jnp.where(live_bool, pressure / (safe_density * safe_density), 0.0)]
  transfers between devices with their start and end apart: 20 -> 0, of which waited for: 11 -> 0; matrix products, arithmetic and copies ran while one was open for 0% -> 0% of each run, Pallas kernels for 0% -> 0%
where the time goes in v1:
time: 108 us; the launch traced here: 106 us
  Pallas kernels  98.6 us (91%)
  local copies, waits for them, and re-layouts  5.59 us (5%)
  other arithmetic  1.43 us (1%)
    pallas_call x1, Pallas kernels, local(): pl.pallas_call(kernel, out_shape=(jax.ShapeDtypeStruct((2, ROWS, COLS, 12...  98.6 us
    unnamed x17, local copies, waits for them, and re-layouts  3.51 us

profile of v1, /device:TPU:1, one launch (start us, length us, event | category | flops | bytes accessed | tf_op | source)
XLA Modules:
  0.0 106.2 jit_solution(10442077657834645267)
XLA Ops:
  0.6 0.0 copy-start.1
  0.6 1.4 %select_convert_fusion.code_ref = f32[6,6,128]{2,1,0:T(8,128)} fusion(s32[6,6,128]{2,1,0:T(8,128)} %param.8, s32[6,6]{1,0:T(8,128)} %param.9), kind=kLoop, calls=%fused_computation | loop fusion | flops 18432 | bytes 37008 | tf_op jit(solution)/shard_map/convert_element_type | solution.py:387
  2.1 0.0 copy-done.1
  2.1 0.0 copy-start.2
  2.1 0.6 copy.9.pos_ref
  2.7 0.1 copy-done.2
  2.8 0.0 copy-start.3
  2.8 0.6 copy.10.vel_ref
  3.5 0.1 copy-done.3
  3.6 0.6 copy.11.oa_ref
  4.2 98.6 %shard_map.84 = (f32[2,6,6,128]{3,2,1,0:T(8,128)}, f32[2,6,6,128]{3,2,1,0:T(8,128)}, f32[6,6,128]{2,1,0:T(8,128)}, f32[4,4]{1,0:T(4,128)}) custom-call(f32[2,6,6,128]{3,2,1,0:T(8,128)} %copy.9.pos_ref, f32[2,6,6,128]{3,2,1,0:T(8,128)} %copy.10.vel_ref, f32[2,6,6,128]{3,2,1,0:T(8,128)} %copy.11.oa_ref, f32[6,6,128]{2,1,0:T(8,128)} %select_convert_fusion.code_ref), custom_call_target="tpu_custom_call" | custom-call | tf_op jit(solution)/shard_map/pallas_call | solution.py:390
  102.8 0.0 copy-start
  102.8 1.4 %copy.12 = f32[2,6,6,128]{3,0,2,1:T(2,128)} copy(f32[2,6,6,128]{3,2,1,0:T(8,128)} %get-tuple-element.4) | data formatting | bytes 73728 | tf_op jit(solution)/shard_map/pallas_call | solution.py:390
  104.3 0.0 copy-done
  104.3 0.0 copy-start.4
  104.3 0.6 copy.13
  104.9 0.1 copy-done.4
  105.0 0.0 copy-start.5
  105.0 0.6 copy.16
  105.6 0.1 copy-done.5
  105.7 0.6 copy.17
Async XLA Ops:
  0.6 1.4 %copy-start.1 = (f32[2,6,6,128]{3,0,2,1:T(2,128)S(1)}, f32[2,6,6,128]{3,0,2,1:T(2,128)}, u32[]{:S(2)}) copy-start(f32[2,6,6,128]{3,0,2,1:T(2,128)} %param.5) | copy-start | bytes 110596
  2.1 0.8 copy-start.2
  2.8 0.8 copy-start.3
  102.8 1.5 %copy-start = (f32[2,6,6,128]{3,2,1,0:T(8,128)S(1)}, f32[2,6,6,128]{3,2,1,0:T(8,128)}, u32[]{:S(2)}) copy-start(f32[2,6,6,128]{3,2,1,0:T(8,128)} %get-tuple-element.5) | copy-start | bytes 110596
  104.3 0.7 copy-start.4
  105.0 0.7 copy-start.5

commit v2 on v1

v2 whole, which is shorter than its diff:
```python
import jax
import jax.numpy as jnp
from jax import lax
from jax.experimental import pallas as pl
from jax.experimental.pallas import tpu as pltpu
from jax.sharding import Mesh
from jax.sharding import PartitionSpec as P

ITERS = 4
TIME_STEP = 0.05
KERNEL_NORM = 4.0 / (3.141592653589793 * 64.0)
REST_LIGHT = 1.2
REST_HEAVY = 1.5
STIFF_LIGHT = 100.0
STIFF_HEAVY = 200.0
MASS_LIGHT = 1.0
MASS_HEAVY = 1.5
FAR = float(2**30)
NEG = -1e30
MESH = pl.DeviceIdType.MESH
SPLIT = ("x", "zl", "zh", "y", "core")
ROWS = 6
COLS = 6
TOP, BOTTOM, LEFT, RIGHT = 0, 7, 8, 9
BLOCKS = 10
FS = BLOCKS * 8
DIRS = ((-1, 0), (1, 0), (0, -1), (0, 1), (-1, -1), (-1, 1), (1, -1), (1, 1))
OWN_TILES = (
    (0, 1, 0, 1, 0), (0, 1, 1, 2, 0),
    (2, 3, 1, 2, 0), (2, 3, 2, 3, 0), (2, 3, 3, 4, 1),
    (4, 5, 3, 4, 1), (4, 5, 4, 5, 1),
    (1, 4, 0, 5, 2),
)
GROUP_START = (0, 2)

f32 = jnp.float32
bf16 = jnp.bfloat16


def rnd(v):
    return v.astype(bf16).astype(f32)


def split3(v):
    h = rnd(v)
    r = v - h
    m = rnd(r)
    return h, m, rnd(r - m)


def feature_rows(x, y):
    xs = split3(x)
    ys = split3(y)
    rs = split3(x * x + y * y)
    one = jnp.ones_like(x)
    zero = jnp.zeros_like(x)
    h, m, l = 0, 1, 2
    jrow = (
        [xs[q] for q in (h, h, m, m, l, h)] + [ys[q] for q in (h, h, m, m, l, h)]
        + list(rs) + [one, one, one] + list(xs) + list(ys) + [one] * 7 + [zero]
    )
    irow = (
        [2.0 * xs[q] for q in (h, m, h, m, h, l)] + [2.0 * ys[q] for q in (h, m, h, m, h, l)]
        + [-one] * 3 + [-q for q in rs] + [zero] * 6 + list(xs) + list(ys) + [zero, zero]
    )
    return jrow, irow


def kernel(
    pos_ref, vel_ref, oa_ref, phase_ref, counts_ref,
    npos_ref, nvel_ref, pres_ref, mon_ref,
    inp, inv, ino, inph, st, xp, tp, stage, tstage, rb, trb, fb, ib, lt, gh, wb, da, fa, tf, mb,
    al, be, ar0, ar1, ar2,
    ins, hs, hr, ts, tr, a1s, a1r, a2s, a2r,
):
    index = {name: lax.axis_index(name) for name in SPLIT}
    size = {name: lax.axis_size(name) for name in SPLIT}
    gx = index["x"] * size["zl"] + index["zl"]
    gy = (index["zh"] * size["y"] + index["y"]) * size["core"] + index["core"]
    nx = size["x"] * size["zl"]
    ny = size["zh"] * size["y"] * size["core"]

    def around(dx, dy):
        px = lax.rem(gx + dx + nx, nx)
        py = lax.rem(gy + dy + ny, ny)
        return (
            px // size["zl"], lax.rem(px, size["zl"]), py // (size["y"] * size["core"]),
            lax.rem(py // size["core"], size["y"]), lax.rem(py, size["core"]),
        )

    def peers(names):
        steps = [()]
        for name in SPLIT:
            count = size[name] if name in names else 1
            steps = [s + (q,) for s in steps for q in range(count)]
        return [
            tuple(lax.rem(index[name] + q, size[name]) for name, q in zip(SPLIT, s))
            for s in steps if any(s)
        ]

    neighbours = [around(dx, dy) for dx, dy in DIRS]
    first_peers = peers(("y", "core"))
    second_peers = peers(("x", "zl", "zh"))
    barrier = pltpu.get_barrier_semaphore()
    for partner in neighbours + first_peers + second_peers:
        pl.semaphore_signal(barrier, inc=1, device_id=partner, device_id_type=MESH)

    loads = [
        pltpu.make_async_copy(src, dst, ins.at[q])
        for q, (src, dst) in enumerate(
            ((pos_ref, inp), (vel_ref, inv), (oa_ref, ino), (phase_ref, inph))
        )
    ]
    for load in loads:
        load.start()

    st[...] = jnp.zeros_like(st)
    da[...] = jnp.zeros_like(da)
    mb[...] = jnp.zeros_like(mb)
    xp[...] = jnp.full_like(xp, FAR)
    tp[...] = jnp.zeros_like(tp)
    fb[...] = jnp.zeros_like(fb)
    stage[...] = jnp.zeros_like(stage)
    tstage[...] = jnp.zeros_like(tstage)
    k = lax.broadcasted_iota(jnp.int32, (16, 128), 0)
    for ox in (-1, 0, 1):
        for oy in (-1, 0, 1):
            o = (ox + 1) * 3 + oy + 1
            al[o] = jnp.where(
                k < 2, 1.0,
                jnp.where((k >= 8) & (k < 11), 2.0 * ox, jnp.where((k >= 11) & (k < 14), 2.0 * oy, 0.0)),
            )
            be[o] = jnp.where(
                (k >= 2) & (k < 5), -2.0 * ox,
                jnp.where(
                    (k >= 5) & (k < 8), -2.0 * oy, jnp.where(k == 14, 1.0 - ox * ox - oy * oy, 0.0)
                ),
            )
    lane = lax.broadcasted_iota(jnp.int32, (1, 128), 1)
    sub = lax.broadcasted_iota(jnp.int32, (8, 128), 0)
    sub_f = sub.astype(f32)
    row_cols = jnp.where(sub == 7, -1.0, sub_f) - 2.5
    for load in loads:
        load.wait()
    for a in range(ROWS):
        for f in range(2):
            for s in range(COLS):
                at = a * 12 + s * 2 + f
                st[f, a, s : s + 1, :] = inp[at : at + 1, :]
                st[2 + f, a, s : s + 1, :] = inv[at : at + 1, :]
                st[9 + f, a, s : s + 1, :] = ino[at : at + 1, :]
        for s in range(COLS):
            st[4, a, s : s + 1, :] = (lane < counts_ref[a, s]).astype(f32)
        st[5, a, 0:COLS, :] = (inph[a] == 1).astype(f32)

    def halo_copies(it, src, staged, dst, send, recv):
        copies = []
        for d in range(8):
            source = src.at[:, (1, ROWS)[d]] if d < 2 else staged.at[d]
            copies.append(
                pltpu.make_async_remote_copy(
                    src_ref=source, dst_ref=dst.at[it, d],
                    send_sem=send.at[it, d], recv_sem=recv.at[it, d],
                    device_id=neighbours[d], device_id_type=MESH,
                )
            )
        return copies

    def pack(src, staged, fields):
        for f in range(fields):
            for a in range(ROWS):
                staged[2, f, a, :] = src[f, a + 1, 0, :]
                staged[3, f, a, :] = src[f, a + 1, COLS - 1, :]
            staged[4, f, 0, :] = src[f, 1, 0, :]
            staged[5, f, 0, :] = src[f, 1, COLS - 1, :]
            staged[6, f, 0, :] = src[f, ROWS, 0, :]
            staged[7, f, 0, :] = src[f, ROWS, COLS - 1, :]

    def unpack(it, dst, got, fields):
        for f in range(fields):
            dst[f, BOTTOM] = got[it, 0, f]
            dst[f, TOP] = got[it, 1, f]
            dst[f, RIGHT] = got[it, 2, f]
            dst[f, LEFT] = got[it, 3, f]
            dst[f, BOTTOM, 6, :] = got[it, 4, f, 0, :]
            dst[f, BOTTOM, 7, :] = got[it, 5, f, 0, :]
            dst[f, TOP, 6, :] = got[it, 6, f, 0, :]
            dst[f, TOP, 7, :] = got[it, 7, f, 0, :]

    def put(buf, rows, base):
        for q, row in enumerate(rows):
            buf[pl.ds(q * FS + base, 8), :] = row

    def cell(buf, c):
        return buf[pl.ds(c, 32, stride=FS), :]

    def turned(cells):
        return jnp.concatenate([cell(fb, c) for c in cells], axis=0).T.astype(bf16)

    def centre(a, col, o):
        base = cell(ib, (a + 1) * 8 + col)
        return jnp.concatenate([base[0:16], base[16:32] * al[o] + be[o]], axis=0).astype(bf16)

    def at_block(part, block, blocks):
        pieces = []
        if block > 0:
            pieces.append(jnp.zeros((32 * block, 128), bf16))
        pieces.append(part)
        if block < blocks - 1:
            pieces.append(jnp.zeros((32 * (blocks - 1 - block), 128), bf16))
        return jnp.concatenate(pieces, axis=0) if len(pieces) > 1 else part

    def overlap(left, right, slot, sums, cols):
        w = jnp.maximum(jnp.dot(left, right, preferred_element_type=f32), 0.0)
        w2 = w * w
        wb[slot] = w2
        part = jnp.sum((w2 * w).reshape(16, 8, 256), axis=0)
        for e in range(2):
            half = part[:, 128 * e : 128 * e + 128]
            sums[cols[e]] = half if sums[cols[e]] is None else sums[cols[e]] + half

    def own_tiles(a, ox3, lrow, slot, sums):
        for q, (ca, cb, ja, jb, group) in enumerate(OWN_TILES):
            pa = centre(a, ca, ox3 + (ja - ca + 1))
            pb = centre(a, cb, ox3 + (jb - cb + 1))
            if group == 2:
                left = jnp.concatenate([lrow[0], lrow[1]], axis=1)
                right = jnp.concatenate([at_block(pa, ja, 8), at_block(pb, jb - 2 + 4, 8)], axis=1)
            else:
                left = lrow[group]
                right = jnp.concatenate(
                    [at_block(pa, ja - GROUP_START[group], 4), at_block(pb, jb - GROUP_START[group], 4)],
                    axis=1,
                )
            overlap(left, right, slot + q, sums, (ca, cb))

    def edge_tile(a, ox3, r, slot, sums):
        pa = centre(a, 0, ox3)
        pb = centre(a, COLS - 1, ox3 + 2)
        odd = (r + 1) % 2
        right = jnp.concatenate([at_block(pa, 2 * odd, 4), at_block(pb, 2 * odd + 1, 4)], axis=1)
        overlap(gh[(r + 1) // 2], right, slot + 8, sums, (0, COLS - 1))

    def pull(w2, left, sums, cols):
        hi = w2.astype(bf16)
        lo = (w2 - hi.astype(f32)).astype(bf16)
        both = jnp.concatenate([left, left], axis=1)
        total = jnp.dot(both, jnp.concatenate([hi, lo], axis=0), preferred_element_type=f32)
        for e in range(2):
            part = total[32 * e : 32 * e + 32, 128 * e : 128 * e + 128]
            sums[cols[e]] = part if sums[cols[e]] is None else sums[cols[e]] + part

    def own_pulls(r, slot, sums):
        for q, (ca, cb, ja, jb, group) in enumerate(OWN_TILES):
            left = jnp.concatenate([tf[r, ja], tf[r, jb]], axis=0)
            pull(wb[slot + q], left, sums, (ca, cb))

    def side_cells(r):
        if r < 0:
            return (TOP, 7), (TOP, 6)
        if r >= ROWS:
            return (BOTTOM, 7), (BOTTOM, 6)
        return (LEFT, r), (RIGHT, r)

    def moment_rows(block, px, py):
        rows = [None] * 32
        for q in range(4):
            field = None if q == 0 else tp[q - 1, block]
            for e, p in enumerate((px, py)):
                pieces = split3(p if field is None else p * field)
                for level in range(3):
                    rows[level * 8 + 2 * q + e] = pieces[level]
            if field is None:
                rows[24], rows[28] = jnp.ones_like(px), jnp.zeros_like(px)
            else:
                rows[24 + q] = rnd(field)
                rows[28 + q] = rnd(field - rows[24 + q])
        return rows

    pl.semaphore_wait(barrier, len(neighbours) + len(first_peers) + len(second_peers))

    def densities(it):
        alive = st[4] > 0.5
        for f in range(2):
            v = st[2 + f] + TIME_STEP * (st[9 + f] + st[7 + f])
            x = st[f] + TIME_STEP * v - 0.5
            xp[f, 1 : ROWS + 1] = jnp.where(alive, x, FAR)
        pack(xp, stage, 2)
        copies = halo_copies(it, xp, stage, rb, hs, hr)
        for copy in copies:
            copy.start()

        for r in range(ROWS):
            jrow, irow = feature_rows(xp[0, r + 1], xp[1, r + 1])
            put(fb, jrow, (r + 1) * 8)
            put(ib, irow, (r + 1) * 8)
        for r in range(ROWS):
            for g in range(2):
                lt[(r + 1) * 2 + g] = turned([(r + 1) * 8 + GROUP_START[g] + s for s in range(4)])
        da[...] = jnp.zeros_like(da)

        def density(t, c):
            a = t // 3
            step = lax.rem(t, 3)
            r = a + step
            sums = [None] * COLS
            own_tiles(a, step * 3, (lt[r * 2], lt[r * 2 + 1]), t * 9, sums)
            for s in range(COLS):
                da[a, s] += sums[s]
            return c

        lax.fori_loop(1, 17, density, 0, unroll=4)

        for copy in copies:
            copy.wait()
        unpack(it, xp, rb, 2)
        for block in (TOP, BOTTOM, LEFT, RIGHT):
            jrow, _ = feature_rows(xp[0, block], xp[1, block])
            put(fb, jrow, block * 8)
        for block in (TOP, BOTTOM):
            for g in range(2):
                lt[block * 2 + g] = turned([block * 8 + GROUP_START[g] + s for s in range(4)])
        for q in range(4):
            cells = [b * 8 + s for r in (2 * q - 1, 2 * q) for b, s in side_cells(r)]
            gh[q] = turned(cells)
        for t in range(18):
            a, ox = t // 3, t % 3 - 1
            r = a + ox
            sums = [None] * COLS
            if r < 0 or r >= ROWS:
                own_tiles(a, (ox + 1) * 3, (lt[(r + 1) * 2], lt[(r + 1) * 2 + 1]), t * 9, sums)
            edge_tile(a, (ox + 1) * 3, r, t * 9, sums)
            for s in range(COLS):
                if sums[s] is not None:
                    da[a, s] += sums[s]

    def bounds_copies(it, src_slot, dst, send, recv, targets):
        return [
            pltpu.make_async_remote_copy(
                src_ref=ar0.at[it, src_slot], dst_ref=dst.at[it, d],
                send_sem=send.at[it, d], recv_sem=recv.at[it, d],
                device_id=target, device_id_type=MESH,
            )
            for d, target in enumerate(targets)
        ]

    def forces(it):
        alive = st[4] > 0.5
        hot = st[5] > 0.5
        rows = []
        for a in range(ROWS):
            cells = [jnp.sum(da[a, s], axis=0, keepdims=True) for s in range(COLS)]
            rows.append(jnp.concatenate(cells + [jnp.zeros((2, 128), f32)], axis=0))
        density_now = KERNEL_NORM * jnp.stack(rows)
        ratio = density_now / jnp.where(hot, REST_HEAVY, REST_LIGHT)
        lit = alive & jnp.logical_not(hot)
        hvy = alive & hot
        peaks = (
            jnp.where(lit, ratio, NEG), jnp.where(hvy, ratio, NEG),
            jnp.where(lit, -ratio, NEG), jnp.where(hvy, -ratio, NEG),
        )
        vec = jnp.full((1, 128), NEG, f32)
        for q in range(4):
            top = jnp.max(jnp.max(peaks[q], axis=0), axis=0, keepdims=True)
            top = jnp.max(top, axis=1, keepdims=True)
            vec = jnp.where(lane == q, top, vec)
        ar0[it, 0] = vec
        first = bounds_copies(it, 0, ar1, a1s, a1r, first_peers)

        safe = jnp.where(alive, density_now, 1.0)
        inverse = 1.0 / (safe * safe)
        excess = jnp.where(hot, STIFF_HEAVY, STIFF_LIGHT) * (ratio - 1.0)
        t0 = jnp.where(alive, st[6] * inverse, 0.0)
        u = excess * inverse
        u0 = jnp.where(lit, u, 0.0)
        u1 = jnp.where(hvy, u, 0.0)
        tp[0, 1 : ROWS + 1] = t0
        tp[1, 1 : ROWS + 1] = u0
        tp[2, 1 : ROWS + 1] = u1
        pack(tp, tstage, 3)
        tcopies = halo_copies(it, tp, tstage, trb, ts, tr)
        for copy in first + tcopies:
            copy.start()

        for a in range(ROWS):
            put(fb, moment_rows(a + 1, xp[0, a + 1] + (a - 2.5), xp[1, a + 1] + row_cols), (a + 1) * 8)
        for a in range(ROWS):
            for s in range(COLS):
                tf[a + 1, s] = cell(fb, (a + 1) * 8 + s).astype(bf16)
        fa[...] = jnp.zeros_like(fa)

        def force(t, c):
            a = t // 3
            step = lax.rem(t, 3)
            sums = [None] * COLS
            own_pulls(a + step, t * 9, sums)
            for s in range(COLS):
                fa[a, s] += sums[s]
            return c

        lax.fori_loop(1, 17, force, 0, unroll=4)

        for copy in first:
            copy.wait()
        best = vec
        for d in range(len(first_peers)):
            best = jnp.maximum(best, ar1[it, d])
        ar0[it, 1] = best
        second = bounds_copies(it, 1, ar2, a2s, a2r, second_peers)
        for copy in second:
            copy.start()

        for copy in tcopies:
            copy.wait()
        unpack(it, tp, trb, 3)
        edge_x = {TOP: -3.5, BOTTOM: 3.5, LEFT: sub_f - 2.5, RIGHT: sub_f - 2.5}
        edge_y = {TOP: row_cols, BOTTOM: row_cols, LEFT: -3.5, RIGHT: 3.5}
        for block in (TOP, BOTTOM, LEFT, RIGHT):
            put(fb, moment_rows(block, xp[0, block] + edge_x[block], xp[1, block] + edge_y[block]), block * 8)
        for block in (TOP, BOTTOM, LEFT, RIGHT):
            for s in range(8 if block in (TOP, BOTTOM) else ROWS):
                tf[block, s] = cell(fb, block * 8 + s).astype(bf16)
        for t in range(18):
            a, ox = t // 3, t % 3 - 1
            r = a + ox
            sums = [None] * COLS
            if r < 0 or r >= ROWS:
                own_pulls(r + 1, t * 9, sums)
            (lb, ls), (rb_, rs_) = side_cells(r)
            pull(
                wb[t * 9 + 8], jnp.concatenate([tf[lb, ls], tf[rb_, rs_]], axis=0), sums, (0, COLS - 1)
            )
            for s in range(COLS):
                if sums[s] is not None:
                    fa[a, s] += sums[s]
        for a in range(ROWS):
            for s in range(COLS):
                part = fa[a, s]
                row = a * 8 + s
                mb[pl.ds(row, 8, stride=FS), :] = part[0:8] + part[8:16] + part[16:24]
                mb[pl.ds(8 * FS + row, 8, stride=FS), :] = part[24:32]

        for copy in second:
            copy.wait()
        for d in range(len(second_peers)):
            best = jnp.maximum(best, ar2[it, d])
        mon_ref[pl.ds(it, 1), :] = jnp.where(lane < 2, best, -best)[:, 0:4]
        relax0 = jnp.broadcast_to(1.0 / (1.0 + best[:, 0:1] + best[:, 2:3]), (8, 128))
        relax1 = jnp.broadcast_to(1.0 / (1.0 + best[:, 1:2] + best[:, 3:4]), (8, 128))

        for a in range(ROWS):
            def mom(q):
                return mb[q * FS + a * 8 : q * FS + a * 8 + 8, :]

            on = alive[a]
            ti = t0[a] + relax0 * u0[a] + relax1 * u1[a]
            s1 = mom(8) + mom(12)
            s_t = (mom(9) + mom(13)) + relax0 * (mom(10) + mom(14)) + relax1 * (mom(11) + mom(15))
            factor = 6.0 * KERNEL_NORM / jnp.where(hot[a], MASS_HEAVY, MASS_LIGHT)
            for f in range(2):
                p = xp[f, a + 1] + (a - 2.5 if f == 0 else row_cols)
                s_p = mom(f)
                s_tp = mom(2 + f) + relax0 * mom(4 + f) + relax1 * mom(6 + f)
                push = ti * (p * s1 - s_p) + p * s_t - s_tp
                st[7 + f, a] = jnp.where(on, factor * push, 0.0)
            relax = jnp.where(hot[a], relax1, relax0)
            st[6, a] = jnp.where(on, st[6, a] + relax * excess[a], 0.0)

    def whole(it, carry):
        densities(it)
        forces(it)
        return carry

    lax.fori_loop(0, ITERS, whole, 0)

    live = st[4]
    for f in range(2):
        v = live * (st[2 + f] + TIME_STEP * (st[9 + f] + st[7 + f]))
        p = live * (st[f] + TIME_STEP * v)
        for a in range(ROWS):
            for s in range(COLS):
                at = a * 12 + s * 2 + f
                nvel_ref[at : at + 1, :] = v[a, s : s + 1]
                npos_ref[at : at + 1, :] = p[a, s : s + 1]
    for a in range(ROWS):
        pres_ref[a] = st[6, a, 0:COLS, :]


def flat(value):
    return value.transpose(1, 2, 0, 3).reshape(ROWS * COLS * 2, 128)


def unflat(value):
    return value.reshape(ROWS, COLS, 2, 128).transpose(2, 0, 1, 3)


def local(position, velocity, other_accel, phase_ids, counts):
    vmem = pl.BlockSpec(memory_space=pltpu.VMEM)
    hbm = pl.BlockSpec(memory_space=pl.ANY)
    dma = pltpu.SemaphoreType.DMA
    n1 = lax.axis_size("y") * lax.axis_size("core") - 1
    n2 = lax.axis_size("x") * lax.axis_size("zl") * lax.axis_size("zh") - 1
    new_pos, new_vel, pressure, monitor = pl.pallas_call(
        kernel,
        out_shape=(
            jax.ShapeDtypeStruct((ROWS * COLS * 2, 128), f32),
            jax.ShapeDtypeStruct((ROWS * COLS * 2, 128), f32),
            jax.ShapeDtypeStruct((ROWS, COLS, 128), f32),
            jax.ShapeDtypeStruct((ITERS, 4), f32),
        ),
        in_specs=[hbm] * 4 + [pl.BlockSpec(memory_space=pltpu.SMEM)],
        out_specs=[vmem] * 4,
        scratch_shapes=[
            pltpu.VMEM((ROWS * COLS * 2, 128), f32),
            pltpu.VMEM((ROWS * COLS * 2, 128), f32),
            pltpu.VMEM((ROWS * COLS * 2, 128), f32),
            pltpu.VMEM((ROWS, COLS, 128), jnp.int32),
            pltpu.VMEM((11, ROWS, 8, 128), f32),
            pltpu.VMEM((2, BLOCKS, 8, 128), f32),
            pltpu.VMEM((3, BLOCKS, 8, 128), f32),
            pltpu.VMEM((8, 2, 8, 128), f32),
            pltpu.VMEM((8, 3, 8, 128), f32),
            pltpu.VMEM((ITERS, 8, 2, 8, 128), f32),
            pltpu.VMEM((ITERS, 8, 3, 8, 128), f32),
            pltpu.VMEM((32 * FS, 128), f32),
            pltpu.VMEM((32 * FS, 128), f32),
            pltpu.VMEM((16, 128, 128), bf16),
            pltpu.VMEM((4, 128, 128), bf16),
            pltpu.VMEM((162, 128, 256), f32),
            pltpu.VMEM((ROWS, COLS, 8, 128), f32),
            pltpu.VMEM((ROWS, COLS, 32, 128), f32),
            pltpu.VMEM((BLOCKS, 8, 32, 128), bf16),
            pltpu.VMEM((16 * FS, 128), f32),
            pltpu.VMEM((9, 16, 128), f32),
            pltpu.VMEM((9, 16, 128), f32),
            pltpu.VMEM((ITERS, 2, 1, 128), f32),
            pltpu.VMEM((ITERS, n1, 1, 128), f32),
            pltpu.VMEM((ITERS, n2, 1, 128), f32),
            dma((4,)),
            dma((ITERS, 8)), dma((ITERS, 8)), dma((ITERS, 8)), dma((ITERS, 8)),
            dma((ITERS, n1)), dma((ITERS, n1)), dma((ITERS, n2)), dma((ITERS, n2)),
        ],
        compiler_params=pltpu.CompilerParams(
            collective_id=0, has_side_effects=True, vmem_limit_bytes=60 * 1024 * 1024
        ),
    )(flat(position), flat(velocity), flat(other_accel), phase_ids, counts)
    return unflat(new_pos), unflat(new_vel), pressure, monitor


def solution(mesh):
    gx = ("x", "zl")
    gy = ("zh", "y", "core")
    torus = Mesh(mesh.devices.reshape(4, 2, 2, 4, 2), SPLIT)
    wide = P(None, gx, gy, None)
    return jax.shard_map(
        local, mesh=torus, in_specs=(wide, wide, wide, P(gx, gy, None), P(gx, gy)),
        out_specs=(wide, wide, P(gx, gy, None), P()), check_vma=False,
    )
```

time: 108 us -> 74.3 us (0.69)
  Pallas kernels: 98.6 us -> 69 us
  local copies, waits for them, and re-layouts: 5.59 us -> 3.39 us
  other arithmetic: 1.43 us -> 0 us
    pallas_call x1, Pallas kernels: 98.6 us -> 69 us  [local(): pl.pallas_call(kernel, out_shape=(jax.ShapeDtypeStruct((ROWS * COLS * 2,...]
    pallas_call x2 -> x0, local copies, waits for them, and re-layouts: 2.08 us -> none  [local(): pl.pallas_call(kernel, out_shape=(jax.ShapeDtypeStruct((2, ROWS, COLS, 12...]
    convert_element_type x1 -> x0, other arithmetic: 1.43 us -> none  [local(): jnp.where(slot[None, None, :] < counts[:, :, None], phase_ids + 1, 0)]
    unnamed x17 -> x10, local copies, waits for them, and re-layouts: 3.51 us -> 3.39 us
where the time goes in v2:
time: 74.3 us; the launch traced here: 73 us
  Pallas kernels  69 us (93%)
  local copies, waits for them, and re-layouts  3.39 us (5%)
    pallas_call x1, Pallas kernels, local(): pl.pallas_call(kernel, out_shape=(jax.ShapeDtypeStruct((ROWS * COLS * 2,...  69 us
    unnamed x10, local copies, waits for them, and re-layouts  3.39 us

profile of v2, /device:TPU:1, one launch (start us, length us, event | category | flops | bytes accessed | tf_op | source)
XLA Modules:
  0.0 73.0 jit_solution(2662922837363185948)
XLA Ops:
  0.6 69.0 %shard_map.84 = (f32[72,128]{1,0:T(8,128)}, f32[72,128]{1,0:T(8,128)}, f32[6,6,128]{2,1,0:T(8,128)}, f32[4,4]{1,0:T(4,128)}) custom-call(f32[72,128]{1,0:T(8,128)} %bitcast.17, f32[72,128]{1,0:T(8,128)} %bitcast.18, f32[72,128]{1,0:T(8,128)} %bitcast.19, s32[6,6,128]{2,1,0:T(8,128)} %phase_ref.1, s32[6,6]{1,0:T(8,128)} %counts_ref.1), custom_call_target="tpu_custom_call" | custom-call | tf_op jit(solution)/shard_map/pallas_call | solution.py:503
  69.6 0.0 copy-start
  69.6 1.4 %copy.13 = f32[2,6,6,128]{3,0,2,1:T(2,128)} copy(f32[2,6,6,128]{3,0,2,1:T(2,128)} %bitcast.16) | data formatting | bytes 73728
  71.0 0.0 copy-done
  71.0 0.0 copy-start.1
  71.0 0.6 copy.14
  71.6 0.1 copy-done.1
  71.8 0.0 copy-start.2
  71.8 0.6 copy.15
  72.4 0.1 copy-done.2
  72.4 0.6 copy.16
Async XLA Ops:
  69.6 1.4 %copy-start = (f32[72,128]{1,0:T(8,128)S(1)}, f32[72,128]{1,0:T(8,128)}, u32[]{:S(2)}) copy-start(f32[72,128]{1,0:T(8,128)} %get-tuple-element.9) | copy-start | bytes 110596
  71.0 0.8 %copy-start.1 = (f32[6,6,128]{2,1,0:T(8,128)S(1)}, f32[6,6,128]{2,1,0:T(8,128)}, u32[]{:S(2)}) copy-start(f32[6,6,128]{2,1,0:T(8,128)} %get-tuple-element.18) | copy-start | bytes 55300
  71.8 0.7 copy-start.2

commit v3 on v2

--- a/solution.py
+++ b/solution.py
@@ -21,8 +21,9 @@
 SPLIT = ("x", "zl", "zh", "y", "core")
 ROWS = 6
 COLS = 6
-TOP, BOTTOM, LEFT, RIGHT = 0, 7, 8, 9
-BLOCKS = 10
+TOP, BOTTOM, LEFT, RIGHT, CORNERS = 0, 7, 8, 9, 10
+EDGES = (TOP, BOTTOM, LEFT, RIGHT)
+BLOCKS = 11
 FS = BLOCKS * 8
 DIRS = ((-1, 0), (1, 0), (0, -1), (0, 1), (-1, -1), (-1, 1), (1, -1), (1, 1))
 OWN_TILES = (
@@ -32,6 +33,11 @@
     (1, 4, 0, 5, 2),
 )
 GROUP_START = (0, 2)
+UNROLL = 4
+OUT_VELOCITY = ROWS * COLS * 2
+OUT_PRESSURE = 2 * OUT_VELOCITY
+OUT_MONITOR = OUT_PRESSURE + ROWS * 8
+OUT_ROWS = OUT_MONITOR + 8
 
 f32 = jnp.float32
 bf16 = jnp.bfloat16
@@ -68,9 +74,9 @@
 
 def kernel(
     pos_ref, vel_ref, oa_ref, phase_ref, counts_ref,
-    npos_ref, nvel_ref, pres_ref, mon_ref,
-    inp, inv, ino, inph, st, xp, tp, stage, tstage, rb, trb, fb, ib, lt, gh, wb, da, fa, tf, mb,
-    al, be, ar0, ar1, ar2,
+    out_ref,
+    inp, inv, ino, inph, st, xp, bp, tp, stage, tstage, cstage, ctstage, rb, trb, crb, ctrb,
+    fb, ib, lt, gh, wb, da, fa, tf, mb, al, be, rl, ar0, ar1, ar2,
     ins, hs, hr, ts, tr, a1s, a1r, a2s, a2r,
 ):
     index = {name: lax.axis_index(name) for name in SPLIT}
@@ -120,8 +126,10 @@
     xp[...] = jnp.full_like(xp, FAR)
     tp[...] = jnp.zeros_like(tp)
     fb[...] = jnp.zeros_like(fb)
-    stage[...] = jnp.zeros_like(stage)
-    tstage[...] = jnp.zeros_like(tstage)
+    bp[...] = jnp.zeros_like(bp)
+    rl[...] = jnp.zeros_like(rl)
+    for buf in (stage, tstage, cstage, ctstage):
+        buf[...] = jnp.zeros_like(buf)
     k = lax.broadcasted_iota(jnp.int32, (16, 128), 0)
     for ox in (-1, 0, 1):
         for oy in (-1, 0, 1):
@@ -148,44 +156,39 @@
                 at = a * 12 + s * 2 + f
                 st[f, a, s : s + 1, :] = inp[at : at + 1, :]
                 st[2 + f, a, s : s + 1, :] = inv[at : at + 1, :]
-                st[9 + f, a, s : s + 1, :] = ino[at : at + 1, :]
+                st[13 + f, a, s : s + 1, :] = ino[at : at + 1, :]
         for s in range(COLS):
             st[4, a, s : s + 1, :] = (lane < counts_ref[a, s]).astype(f32)
         st[5, a, 0:COLS, :] = (inph[a] == 1).astype(f32)
 
-    def halo_copies(it, src, staged, dst, send, recv):
-        copies = []
+    def halo_copies(src, staged, corners, dst, cdst, send, recv):
+        edges = []
+        diagonals = []
         for d in range(8):
-            source = src.at[:, (1, ROWS)[d]] if d < 2 else staged.at[d]
-            copies.append(
+            if d < 4:
+                source = src.at[:, (1, ROWS)[d]] if d < 2 else staged.at[d - 2]
+                target = dst.at[d]
+            else:
+                source, target = corners.at[d - 4], cdst.at[d - 4]
+            (edges if d < 4 else diagonals).append(
                 pltpu.make_async_remote_copy(
-                    src_ref=source, dst_ref=dst.at[it, d],
-                    send_sem=send.at[it, d], recv_sem=recv.at[it, d],
+                    src_ref=source, dst_ref=target, send_sem=send.at[d], recv_sem=recv.at[d],
                     device_id=neighbours[d], device_id_type=MESH,
                 )
             )
-        return copies
-
-    def pack(src, staged, fields):
+        return diagonals, edges
+
+    def pack(src, staged, corners, fields):
         for f in range(fields):
+            corners[0, f : f + 1, :] = src[f, 1, 0:1, :]
+            corners[1, f : f + 1, :] = src[f, 1, COLS - 1 : COLS, :]
+            corners[2, f : f + 1, :] = src[f, ROWS, 0:1, :]
+            corners[3, f : f + 1, :] = src[f, ROWS, COLS - 1 : COLS, :]
             for a in range(ROWS):
-                staged[2, f, a, :] = src[f, a + 1, 0, :]
-                staged[3, f, a, :] = src[f, a + 1, COLS - 1, :]
-            staged[4, f, 0, :] = src[f, 1, 0, :]
-            staged[5, f, 0, :] = src[f, 1, COLS - 1, :]
-            staged[6, f, 0, :] = src[f, ROWS, 0, :]
-            staged[7, f, 0, :] = src[f, ROWS, COLS - 1, :]
-
-    def unpack(it, dst, got, fields):
-        for f in range(fields):
-            dst[f, BOTTOM] = got[it, 0, f]
-            dst[f, TOP] = got[it, 1, f]
-            dst[f, RIGHT] = got[it, 2, f]
-            dst[f, LEFT] = got[it, 3, f]
-            dst[f, BOTTOM, 6, :] = got[it, 4, f, 0, :]
-            dst[f, BOTTOM, 7, :] = got[it, 5, f, 0, :]
-            dst[f, TOP, 6, :] = got[it, 6, f, 0, :]
-            dst[f, TOP, 7, :] = got[it, 7, f, 0, :]
+                staged[0, f, a : a + 1, :] = src[f, a + 1, 0:1, :]
+                staged[1, f, a : a + 1, :] = src[f, a + 1, COLS - 1 : COLS, :]
+
+    PLACE = (3, 2, 1, 0)
 
     def put(buf, rows, base):
         for q, row in enumerate(rows):
@@ -237,9 +240,9 @@
     def edge_tile(a, ox3, r, slot, sums):
         pa = centre(a, 0, ox3)
         pb = centre(a, COLS - 1, ox3 + 2)
-        odd = (r + 1) % 2
+        group, odd = divmod(r, 2) if 0 <= r < ROWS else (3, int(r >= ROWS))
         right = jnp.concatenate([at_block(pa, 2 * odd, 4), at_block(pb, 2 * odd + 1, 4)], axis=1)
-        overlap(gh[(r + 1) // 2], right, slot + 8, sums, (0, COLS - 1))
+        overlap(gh[group], right, slot + 8, sums, (0, COLS - 1))
 
     def pull(w2, left, sums, cols):
         hi = w2.astype(bf16)
@@ -257,9 +260,9 @@
 
     def side_cells(r):
         if r < 0:
-            return (TOP, 7), (TOP, 6)
+            return (CORNERS, 0), (CORNERS, 1)
         if r >= ROWS:
-            return (BOTTOM, 7), (BOTTOM, 6)
+            return (CORNERS, 2), (CORNERS, 3)
         return (LEFT, r), (RIGHT, r)
 
     def moment_rows(block, px, py):
@@ -279,17 +282,46 @@
 
     pl.semaphore_wait(barrier, len(neighbours) + len(first_peers) + len(second_peers))
 
-    def densities(it):
+    position_copies = halo_copies(bp, stage, cstage, rb, crb, hs, hr)
+    term_copies = halo_copies(tp, tstage, ctstage, trb, ctrb, ts, tr)
+
+    def start(pair):
+        for copy in pair[0] + pair[1]:
+            copy.start()
+
+    def coefficients():
         alive = st[4] > 0.5
         for f in range(2):
-            v = st[2 + f] + TIME_STEP * (st[9 + f] + st[7 + f])
-            x = st[f] + TIME_STEP * v - 0.5
-            xp[f, 1 : ROWS + 1] = jnp.where(alive, x, FAR)
-        pack(xp, stage, 2)
-        copies = halo_copies(it, xp, stage, rb, hs, hr)
-        for copy in copies:
-            copy.start()
-
+            free = st[f] + TIME_STEP * (st[2 + f] + TIME_STEP * st[13 + f]) - 0.5
+            step = TIME_STEP * TIME_STEP
+            bp[3 * f, 1 : ROWS + 1] = jnp.where(alive, free + step * st[7 + 3 * f], FAR)
+            bp[3 * f + 1, 1 : ROWS + 1] = step * st[8 + 3 * f]
+            bp[3 * f + 2, 1 : ROWS + 1] = step * st[9 + 3 * f]
+        pack(bp, stage, cstage, 6)
+        start(position_copies)
+
+    def side_tiles(which):
+        done = []
+        for t in range(18):
+            a, ox = t // 3, t % 3 - 1
+            r = a + ox
+            outside = r < 0 or r >= ROWS
+            if which == "edges" and outside:
+                done.append((t, a, ox, r, True))
+            if outside == (which == "corners"):
+                done.append((t, a, ox, r, False))
+        return done
+
+    def add_up(buf, a, sums):
+        for s in range(COLS):
+            if sums[s] is not None:
+                buf[a, s] += sums[s]
+
+    def densities(it):
+        relax0, relax1 = rl[0], rl[1]
+        for f in range(2):
+            for r in range(ROWS):
+                xp[f, r + 1] = bp[3 * f, r + 1] + relax0 * bp[3 * f + 1, r + 1] + relax1 * bp[3 * f + 2, r + 1]
         for r in range(ROWS):
             jrow, irow = feature_rows(xp[0, r + 1], xp[1, r + 1])
             put(fb, jrow, (r + 1) * 8)
@@ -309,42 +341,58 @@
                 da[a, s] += sums[s]
             return c
 
-        lax.fori_loop(1, 17, density, 0, unroll=4)
-
-        for copy in copies:
+        lax.fori_loop(1, 17, density, 0, unroll=UNROLL)
+
+        diagonals, edges = position_copies
+        for copy in edges:
             copy.wait()
-        unpack(it, xp, rb, 2)
-        for block in (TOP, BOTTOM, LEFT, RIGHT):
+        for d, block in enumerate((BOTTOM, TOP, RIGHT, LEFT)):
+            for f in range(2):
+                xp[f, block] = rb[d, 3 * f] + relax0 * rb[d, 3 * f + 1] + relax1 * rb[d, 3 * f + 2]
+        for block in EDGES:
             jrow, _ = feature_rows(xp[0, block], xp[1, block])
             put(fb, jrow, block * 8)
         for block in (TOP, BOTTOM):
             for g in range(2):
                 lt[block * 2 + g] = turned([block * 8 + GROUP_START[g] + s for s in range(4)])
-        for q in range(4):
-            cells = [b * 8 + s for r in (2 * q - 1, 2 * q) for b, s in side_cells(r)]
-            gh[q] = turned(cells)
-        for t in range(18):
-            a, ox = t // 3, t % 3 - 1
-            r = a + ox
+        for q in range(3):
+            gh[q] = turned([b * 8 + s for r in (2 * q, 2 * q + 1) for b, s in side_cells(r)])
+        for t, a, ox, r, row in side_tiles("edges"):
             sums = [None] * COLS
-            if r < 0 or r >= ROWS:
+            if row:
                 own_tiles(a, (ox + 1) * 3, (lt[(r + 1) * 2], lt[(r + 1) * 2 + 1]), t * 9, sums)
+            else:
+                edge_tile(a, (ox + 1) * 3, r, t * 9, sums)
+            add_up(da, a, sums)
+
+        for copy in diagonals:
+            copy.wait()
+        for d in range(4):
+            for f in range(2):
+                xp[f, CORNERS, PLACE[d] : PLACE[d] + 1, :] = (
+                    crb[d, 3 * f : 3 * f + 1, :] + relax0[0:1] * crb[d, 3 * f + 1 : 3 * f + 2, :]
+                    + relax1[0:1] * crb[d, 3 * f + 2 : 3 * f + 3, :]
+                )
+        jrow, _ = feature_rows(xp[0, CORNERS], xp[1, CORNERS])
+        put(fb, jrow, CORNERS * 8)
+        gh[3] = turned([CORNERS * 8 + q for q in range(4)])
+        for t, a, ox, r, row in side_tiles("corners"):
+            sums = [None] * COLS
             edge_tile(a, (ox + 1) * 3, r, t * 9, sums)
-            for s in range(COLS):
-                if sums[s] is not None:
-                    da[a, s] += sums[s]
-
-    def bounds_copies(it, src_slot, dst, send, recv, targets):
+            add_up(da, a, sums)
+
+    def bounds_copies(now, src_slot, dst, send, recv, targets):
         return [
             pltpu.make_async_remote_copy(
-                src_ref=ar0.at[it, src_slot], dst_ref=dst.at[it, d],
-                send_sem=send.at[it, d], recv_sem=recv.at[it, d],
+                src_ref=ar0.at[now, src_slot], dst_ref=dst.at[now, d],
+                send_sem=send.at[now, d], recv_sem=recv.at[now, d],
                 device_id=target, device_id_type=MESH,
             )
             for d, target in enumerate(targets)
         ]
 
     def forces(it):
+        now = lax.rem(it, 2)
         alive = st[4] > 0.5
         hot = st[5] > 0.5
         rows = []
@@ -364,8 +412,8 @@
             top = jnp.max(jnp.max(peaks[q], axis=0), axis=0, keepdims=True)
             top = jnp.max(top, axis=1, keepdims=True)
             vec = jnp.where(lane == q, top, vec)
-        ar0[it, 0] = vec
-        first = bounds_copies(it, 0, ar1, a1s, a1r, first_peers)
+        ar0[now, 0] = vec
+        first = bounds_copies(now, 0, ar1, a1s, a1r, first_peers)
 
         safe = jnp.where(alive, density_now, 1.0)
         inverse = 1.0 / (safe * safe)
@@ -377,10 +425,10 @@
         tp[0, 1 : ROWS + 1] = t0
         tp[1, 1 : ROWS + 1] = u0
         tp[2, 1 : ROWS + 1] = u1
-        pack(tp, tstage, 3)
-        tcopies = halo_copies(it, tp, tstage, trb, ts, tr)
-        for copy in first + tcopies:
+        pack(tp, tstage, ctstage, 3)
+        for copy in first:
             copy.start()
+        start(term_copies)
 
         for a in range(ROWS):
             put(fb, moment_rows(a + 1, xp[0, a + 1] + (a - 2.5), xp[1, a + 1] + row_cols), (a + 1) * 8)
@@ -398,41 +446,59 @@
                 fa[a, s] += sums[s]
             return c
 
-        lax.fori_loop(1, 17, force, 0, unroll=4)
+        lax.fori_loop(1, 17, force, 0, unroll=UNROLL)
 
         for copy in first:
             copy.wait()
         best = vec
         for d in range(len(first_peers)):
-            best = jnp.maximum(best, ar1[it, d])
-        ar0[it, 1] = best
-        second = bounds_copies(it, 1, ar2, a2s, a2r, second_peers)
+            best = jnp.maximum(best, ar1[now, d])
+        ar0[now, 1] = best
+        second = bounds_copies(now, 1, ar2, a2s, a2r, second_peers)
         for copy in second:
             copy.start()
 
-        for copy in tcopies:
+        diagonals, edges = term_copies
+        for copy in edges:
             copy.wait()
-        unpack(it, tp, trb, 3)
+        for d, block in enumerate((BOTTOM, TOP, RIGHT, LEFT)):
+            for f in range(3):
+                tp[f, block] = trb[d, f]
         edge_x = {TOP: -3.5, BOTTOM: 3.5, LEFT: sub_f - 2.5, RIGHT: sub_f - 2.5}
         edge_y = {TOP: row_cols, BOTTOM: row_cols, LEFT: -3.5, RIGHT: 3.5}
-        for block in (TOP, BOTTOM, LEFT, RIGHT):
+        for block in EDGES:
             put(fb, moment_rows(block, xp[0, block] + edge_x[block], xp[1, block] + edge_y[block]), block * 8)
-        for block in (TOP, BOTTOM, LEFT, RIGHT):
-            for s in range(8 if block in (TOP, BOTTOM) else ROWS):
+        for block in EDGES:
+            for s in range(ROWS):
                 tf[block, s] = cell(fb, block * 8 + s).astype(bf16)
-        for t in range(18):
-            a, ox = t // 3, t % 3 - 1
-            r = a + ox
+
+        def side_pull(t, r, sums):
+            (lb, ls), (ub, us) = side_cells(r)
+            pull(wb[t * 9 + 8], jnp.concatenate([tf[lb, ls], tf[ub, us]], axis=0), sums, (0, COLS - 1))
+
+        for t, a, ox, r, row in side_tiles("edges"):
             sums = [None] * COLS
-            if r < 0 or r >= ROWS:
+            if row:
                 own_pulls(r + 1, t * 9, sums)
-            (lb, ls), (rb_, rs_) = side_cells(r)
-            pull(
-                wb[t * 9 + 8], jnp.concatenate([tf[lb, ls], tf[rb_, rs_]], axis=0), sums, (0, COLS - 1)
-            )
-            for s in range(COLS):
-                if sums[s] is not None:
-                    fa[a, s] += sums[s]
+            else:
+                side_pull(t, r, sums)
+            add_up(fa, a, sums)
+
+        for copy in diagonals:
+            copy.wait()
+        for d in range(4):
+            for f in range(3):
+                tp[f, CORNERS, PLACE[d] : PLACE[d] + 1, :] = ctrb[d, f : f + 1, :]
+        corner_x = jnp.where(sub < 2, -3.5, 3.5)
+        corner_y = jnp.where(lax.rem(sub, 2) == 0, -3.5, 3.5)
+        put(fb, moment_rows(CORNERS, xp[0, CORNERS] + corner_x, xp[1, CORNERS] + corner_y), CORNERS * 8)
+        for s in range(4):
+            tf[CORNERS, s] = cell(fb, CORNERS * 8 + s).astype(bf16)
+        for t, a, ox, r, row in side_tiles("corners"):
+            sums = [None] * COLS
+            side_pull(t, r, sums)
+            add_up(fa, a, sums)
+
         for a in range(ROWS):
             for s in range(COLS):
                 part = fa[a, s]
@@ -440,31 +506,39 @@
                 mb[pl.ds(row, 8, stride=FS), :] = part[0:8] + part[8:16] + part[16:24]
                 mb[pl.ds(8 * FS + row, 8, stride=FS), :] = part[24:32]
 
+        for a in range(ROWS):
+            def mom(q):
+                return mb[q * FS + a * 8 : q * FS + a * 8 + 8, :]
+
+            s1 = mom(8) + mom(12)
+            factor = jnp.where(
+                alive[a], 6.0 * KERNEL_NORM / jnp.where(hot[a], MASS_HEAVY, MASS_LIGHT), 0.0
+            )
+            for f in range(2):
+                p = xp[f, a + 1] + (a - 2.5 if f == 0 else row_cols)
+                arm = p * s1 - mom(f)
+                for q, term in enumerate((t0[a], u0[a], u1[a])):
+                    push = term * arm + p * (mom(9 + q) + mom(13 + q)) - mom(2 + 2 * q + f)
+                    st[7 + 3 * f + q, a] = jnp.where(alive[a], factor * push, 0.0)
+
+        @pl.when(it < ITERS - 1)
+        def _():
+            coefficients()
+
         for copy in second:
             copy.wait()
         for d in range(len(second_peers)):
-            best = jnp.maximum(best, ar2[it, d])
-        mon_ref[pl.ds(it, 1), :] = jnp.where(lane < 2, best, -best)[:, 0:4]
+            best = jnp.maximum(best, ar2[now, d])
+        out_ref[pl.ds(OUT_MONITOR + it, 1), :] = jnp.where(lane < 2, best, -best)
         relax0 = jnp.broadcast_to(1.0 / (1.0 + best[:, 0:1] + best[:, 2:3]), (8, 128))
         relax1 = jnp.broadcast_to(1.0 / (1.0 + best[:, 1:2] + best[:, 3:4]), (8, 128))
-
+        rl[0] = relax0
+        rl[1] = relax1
         for a in range(ROWS):
-            def mom(q):
-                return mb[q * FS + a * 8 : q * FS + a * 8 + 8, :]
-
-            on = alive[a]
-            ti = t0[a] + relax0 * u0[a] + relax1 * u1[a]
-            s1 = mom(8) + mom(12)
-            s_t = (mom(9) + mom(13)) + relax0 * (mom(10) + mom(14)) + relax1 * (mom(11) + mom(15))
-            factor = 6.0 * KERNEL_NORM / jnp.where(hot[a], MASS_HEAVY, MASS_LIGHT)
-            for f in range(2):
-                p = xp[f, a + 1] + (a - 2.5 if f == 0 else row_cols)
-                s_p = mom(f)
-                s_tp = mom(2 + f) + relax0 * mom(4 + f) + relax1 * mom(6 + f)
-                push = ti * (p * s1 - s_p) + p * s_t - s_tp
-                st[7 + f, a] = jnp.where(on, factor * push, 0.0)
             relax = jnp.where(hot[a], relax1, relax0)
-            st[6, a] = jnp.where(on, st[6, a] + relax * excess[a], 0.0)
+            st[6, a] = jnp.where(alive[a], st[6, a] + relax * excess[a], 0.0)
+
+    coefficients()
 
     def whole(it, carry):
         densities(it)
@@ -473,17 +547,23 @@
 
     lax.fori_loop(0, ITERS, whole, 0)
 
-    live = st[4]
-    for f in range(2):
-        v = live * (st[2 + f] + TIME_STEP * (st[9 + f] + st[7 + f]))
-        p = live * (st[f] + TIME_STEP * v)
-        for a in range(ROWS):
-            for s in range(COLS):
-                at = a * 12 + s * 2 + f
-                nvel_ref[at : at + 1, :] = v[a, s : s + 1]
-                npos_ref[at : at + 1, :] = p[a, s : s + 1]
     for a in range(ROWS):
-        pres_ref[a] = st[6, a, 0:COLS, :]
+        live = st[4, a]
+        for f in range(2):
+            accel = st[7 + 3 * f, a] + rl[0] * st[8 + 3 * f, a] + rl[1] * st[9 + 3 * f, a]
+            v = live * (st[2 + f, a] + TIME_STEP * (st[13 + f, a] + accel))
+            p = live * (st[f, a] + TIME_STEP * v)
+            out_ref[pl.ds(a * 12 + f, COLS, stride=2), :] = p[0:COLS]
+            out_ref[pl.ds(OUT_VELOCITY + a * 12 + f, COLS, stride=2), :] = v[0:COLS]
+        out_ref[OUT_PRESSURE + a * 8 : OUT_PRESSURE + a * 8 + 8, :] = st[6, a]
+
+
+def spread(in_ref, npos_ref, nvel_ref, pres_ref, mon_ref):
+    npos_ref[...] = in_ref[0:OUT_VELOCITY, :]
+    nvel_ref[...] = in_ref[OUT_VELOCITY:OUT_PRESSURE, :]
+    for a in range(ROWS):
+        pres_ref[a] = in_ref[OUT_PRESSURE + a * 8 : OUT_PRESSURE + a * 8 + COLS, :]
+    mon_ref[...] = in_ref[OUT_MONITOR : OUT_MONITOR + ITERS, 0:4]
 
 
 def flat(value):
@@ -500,28 +580,28 @@
     dma = pltpu.SemaphoreType.DMA
     n1 = lax.axis_size("y") * lax.axis_size("core") - 1
     n2 = lax.axis_size("x") * lax.axis_size("zl") * lax.axis_size("zh") - 1
-    new_pos, new_vel, pressure, monitor = pl.pallas_call(
+    packed = pl.pallas_call(
         kernel,
-        out_shape=(
-            jax.ShapeDtypeStruct((ROWS * COLS * 2, 128), f32),
-            jax.ShapeDtypeStruct((ROWS * COLS * 2, 128), f32),
-            jax.ShapeDtypeStruct((ROWS, COLS, 128), f32),
-            jax.ShapeDtypeStruct((ITERS, 4), f32),
-        ),
+        out_shape=jax.ShapeDtypeStruct((OUT_ROWS, 128), f32),
         in_specs=[hbm] * 4 + [pl.BlockSpec(memory_space=pltpu.SMEM)],
-        out_specs=[vmem] * 4,
+        out_specs=vmem,
         scratch_shapes=[
             pltpu.VMEM((ROWS * COLS * 2, 128), f32),
             pltpu.VMEM((ROWS * COLS * 2, 128), f32),
             pltpu.VMEM((ROWS * COLS * 2, 128), f32),
             pltpu.VMEM((ROWS, COLS, 128), jnp.int32),
-            pltpu.VMEM((11, ROWS, 8, 128), f32),
+            pltpu.VMEM((15, ROWS, 8, 128), f32),
             pltpu.VMEM((2, BLOCKS, 8, 128), f32),
+            pltpu.VMEM((6, BLOCKS, 8, 128), f32),
             pltpu.VMEM((3, BLOCKS, 8, 128), f32),
-            pltpu.VMEM((8, 2, 8, 128), f32),
-            pltpu.VMEM((8, 3, 8, 128), f32),
-            pltpu.VMEM((ITERS, 8, 2, 8, 128), f32),
-            pltpu.VMEM((ITERS, 8, 3, 8, 128), f32),
+            pltpu.VMEM((2, 6, 8, 128), f32),
+            pltpu.VMEM((2, 3, 8, 128), f32),
+            pltpu.VMEM((4, 8, 128), f32),
+            pltpu.VMEM((4, 8, 128), f32),
+            pltpu.VMEM((4, 6, 8, 128), f32),
+            pltpu.VMEM((4, 3, 8, 128), f32),
+            pltpu.VMEM((4, 8, 128), f32),
+            pltpu.VMEM((4, 8, 128), f32),
             pltpu.VMEM((32 * FS, 128), f32),
             pltpu.VMEM((32 * FS, 128), f32),
             pltpu.VMEM((16, 128, 128), bf16),
@@ -533,17 +613,29 @@
             pltpu.VMEM((16 * FS, 128), f32),
             pltpu.VMEM((9, 16, 128), f32),
             pltpu.VMEM((9, 16, 128), f32),
-            pltpu.VMEM((ITERS, 2, 1, 128), f32),
-            pltpu.VMEM((ITERS, n1, 1, 128), f32),
-            pltpu.VMEM((ITERS, n2, 1, 128), f32),
-            dma((4,)),
-            dma((ITERS, 8)), dma((ITERS, 8)), dma((ITERS, 8)), dma((ITERS, 8)),
-            dma((ITERS, n1)), dma((ITERS, n1)), dma((ITERS, n2)), dma((ITERS, n2)),
+            pltpu.VMEM((2, 8, 128), f32),
+            pltpu.VMEM((2, 2, 1, 128), f32),
+            pltpu.VMEM((2, n1, 1, 128), f32),
+            pltpu.VMEM((2, n2, 1, 128), f32),
+            dma((4,)), dma((8,)), dma((8,)), dma((8,)), dma((8,)),
+            dma((2, n1)), dma((2, n1)), dma((2, n2)), dma((2, n2)),
         ],
         compiler_params=pltpu.CompilerParams(
-            collective_id=0, has_side_effects=True, vmem_limit_bytes=60 * 1024 * 1024
+            collective_id=0, has_side_effects=True, vmem_limit_bytes=36 * 1024 * 1024
         ),
     )(flat(position), flat(velocity), flat(other_accel), phase_ids, counts)
+    new_pos, new_vel, pressure, monitor = pl.pallas_call(
+        spread,
+        out_shape=(
+            jax.ShapeDtypeStruct((ROWS * COLS * 2, 128), f32),
+            jax.ShapeDtypeStruct((ROWS * COLS * 2, 128), f32),
+            jax.ShapeDtypeStruct((ROWS, COLS, 128), f32),
+            jax.ShapeDtypeStruct((ITERS, 4), f32),
+        ),
+        in_specs=[vmem],
+        out_specs=[vmem] * 4,
+        compiler_params=pltpu.CompilerParams(vmem_limit_bytes=4 * 1024 * 1024),
+    )(packed)
     return unflat(new_pos), unflat(new_vel), pressure, monitor
 
 

time: 74.3 us -> 68.9 us (0.927)
  Pallas kernels: 69 us -> 63.5 us
    pallas_call x1 -> x2, Pallas kernels: 69 us -> 63.5 us  [the longest x1 62.8 us: local(): pl.pallas_call(kernel, out_shape=jax.ShapeDtypeStruct((OUT_ROWS, 128), f3...]
where the time goes in v3:
time: 68.9 us; the launch traced here: 67.9 us
  Pallas kernels  63.5 us (92%)
  local copies, waits for them, and re-layouts  3.72 us (5%)
    pallas_call x1, Pallas kernels, local(): pl.pallas_call(kernel, out_shape=jax.ShapeDtypeStruct((OUT_ROWS, 128), f3...  62.8 us
    unnamed x10, local copies, waits for them, and re-layouts  3.72 us

profile of v3, /device:TPU:1, one launch (start us, length us, event | category | flops | bytes accessed | tf_op | source)
XLA Modules:
  0.0 67.9 jit_solution(11565038102175430930)
XLA Ops:
  0.6 0.0 copy-start.4
  0.6 0.7 copy-done.4
  1.3 0.0 copy-start
  1.3 0.8 %copy-done = f32[2,6,6,128]{3,0,2,1:T(2,128)S(1)} copy-done((f32[2,6,6,128]{3,0,2,1:T(2,128)S(1)}, f32[2,6,6,128]{3,0,2,1:T(2,128)}, u32[]{:S(2)}) %copy-start) | copy-done | bytes 36888
  2.1 0.0 copy-start.1
  2.1 0.8 %copy-done.1 = f32[2,6,6,128]{3,0,2,1:T(2,128)S(1)} copy-done((f32[2,6,6,128]{3,0,2,1:T(2,128)S(1)}, f32[2,6,6,128]{3,0,2,1:T(2,128)}, u32[]{:S(2)}) %copy-start.1) | copy-done | bytes 36888
  2.9 0.0 copy-start.2
  2.9 0.8 %copy-done.2 = f32[2,6,6,128]{3,0,2,1:T(2,128)S(1)} copy-done((f32[2,6,6,128]{3,0,2,1:T(2,128)S(1)}, f32[2,6,6,128]{3,0,2,1:T(2,128)}, u32[]{:S(2)}) %copy-start.2) | copy-done | bytes 36888
  3.6 0.0 copy-start.3
  3.6 0.7 %copy-done.3 = s32[6,6,128]{2,1,0:T(8,128)S(1)} copy-done((s32[6,6,128]{2,1,0:T(8,128)S(1)}, s32[6,6,128]{2,1,0:T(8,128)}, u32[]{:S(2)}) %copy-start.3) | copy-done | bytes 18456
  4.4 62.8 %shard_map.84.in_ref = f32[200,128]{1,0:T(8,128)S(1)} custom-call(f32[72,128]{1,0:T(8,128)S(1)} %bitcast.15, f32[72,128]{1,0:T(8,128)S(1)} %bitcast.16, f32[72,128]{1,0:T(8,128)S(1)} %bitcast.17, s32[6,6,128]{2,1,0:T(8,128)S(1)} %copy-done.3, s32[6,6]{1,0:T(8,128)S(1)} %copy-done.4), custom_call_target="tpu_custom_call" | custom-call | tf_op jit(solution)/shard_map/pallas_call | solution.py:583
  67.2 0.6 shard_map.85
Async XLA Ops:
  0.6 0.7 %copy-start.4 = (s32[6,6]{1,0:T(8,128)S(1)}, s32[6,6]{1,0:T(8,128)}, u32[]{:S(2)}) copy-start(s32[6,6]{1,0:T(8,128)} %counts_ref.1) | copy-start | bytes 436
  1.3 0.8 %copy-start = (f32[2,6,6,128]{3,0,2,1:T(2,128)S(1)}, f32[2,6,6,128]{3,0,2,1:T(2,128)}, u32[]{:S(2)}) copy-start(f32[2,6,6,128]{3,0,2,1:T(2,128)} %param.5) | copy-start | bytes 110596
  2.1 0.8 %copy-start.1 = (f32[2,6,6,128]{3,0,2,1:T(2,128)S(1)}, f32[2,6,6,128]{3,0,2,1:T(2,128)}, u32[]{:S(2)}) copy-start(f32[2,6,6,128]{3,0,2,1:T(2,128)} %param.6) | copy-start | bytes 110596
  2.9 0.8 %copy-start.2 = (f32[2,6,6,128]{3,0,2,1:T(2,128)S(1)}, f32[2,6,6,128]{3,0,2,1:T(2,128)}, u32[]{:S(2)}) copy-start(f32[2,6,6,128]{3,0,2,1:T(2,128)} %param.7) | copy-start | bytes 110596
  3.6 0.7 %copy-start.3 = (s32[6,6,128]{2,1,0:T(8,128)S(1)}, s32[6,6,128]{2,1,0:T(8,128)}, u32[]{:S(2)}) copy-start(s32[6,6,128]{2,1,0:T(8,128)} %phase_ref.1) | copy-start | bytes 55300

commit v4 on v3

--- a/solution.py
+++ b/solution.py
@@ -33,7 +33,7 @@
     (1, 4, 0, 5, 2),
 )
 GROUP_START = (0, 2)
-UNROLL = 4
+UNROLL = 8
 OUT_VELOCITY = ROWS * COLS * 2
 OUT_PRESSURE = 2 * OUT_VELOCITY
 OUT_MONITOR = OUT_PRESSURE + ROWS * 8
@@ -198,7 +198,7 @@
         return buf[pl.ds(c, 32, stride=FS), :]
 
     def turned(cells):
-        return jnp.concatenate([cell(fb, c) for c in cells], axis=0).T.astype(bf16)
+        return jnp.concatenate([cell(fb, c) for c in cells], axis=0).astype(bf16).T
 
     def centre(a, col, o):
         base = cell(ib, (a + 1) * 8 + col)
@@ -338,7 +338,7 @@
             sums = [None] * COLS
             own_tiles(a, step * 3, (lt[r * 2], lt[r * 2 + 1]), t * 9, sums)
             for s in range(COLS):
-                da[a, s] += sums[s]
+                da[pl.ds(a * 64 + s * 8, 8), :] += sums[s]
             return c
 
         lax.fori_loop(1, 17, density, 0, unroll=UNROLL)
@@ -363,7 +363,9 @@
                 own_tiles(a, (ox + 1) * 3, (lt[(r + 1) * 2], lt[(r + 1) * 2 + 1]), t * 9, sums)
             else:
                 edge_tile(a, (ox + 1) * 3, r, t * 9, sums)
-            add_up(da, a, sums)
+            for s in range(COLS):
+                if sums[s] is not None:
+                    da[a * 64 + s * 8 : a * 64 + s * 8 + 8, :] += sums[s]
 
         for copy in diagonals:
             copy.wait()
@@ -379,7 +381,9 @@
         for t, a, ox, r, row in side_tiles("corners"):
             sums = [None] * COLS
             edge_tile(a, (ox + 1) * 3, r, t * 9, sums)
-            add_up(da, a, sums)
+            for s in range(COLS):
+                if sums[s] is not None:
+                    da[a * 64 + s * 8 : a * 64 + s * 8 + 8, :] += sums[s]
 
     def bounds_copies(now, src_slot, dst, send, recv, targets):
         return [
@@ -397,8 +401,10 @@
         hot = st[5] > 0.5
         rows = []
         for a in range(ROWS):
-            cells = [jnp.sum(da[a, s], axis=0, keepdims=True) for s in range(COLS)]
-            rows.append(jnp.concatenate(cells + [jnp.zeros((2, 128), f32)], axis=0))
+            parts = [da[pl.ds(a * 64 + q, 8, stride=8), :] for q in range(8)]
+            while len(parts) > 1:
+                parts = [parts[q] + parts[q + 1] for q in range(0, len(parts), 2)]
+            rows.append(parts[0])
         density_now = KERNEL_NORM * jnp.stack(rows)
         ratio = density_now / jnp.where(hot, REST_HEAVY, REST_LIGHT)
         lit = alive & jnp.logical_not(hot)
@@ -414,6 +420,8 @@
             vec = jnp.where(lane == q, top, vec)
         ar0[now, 0] = vec
         first = bounds_copies(now, 0, ar1, a1s, a1r, first_peers)
+        for copy in first:
+            copy.start()
 
         safe = jnp.where(alive, density_now, 1.0)
         inverse = 1.0 / (safe * safe)
@@ -426,8 +434,6 @@
         tp[1, 1 : ROWS + 1] = u0
         tp[2, 1 : ROWS + 1] = u1
         pack(tp, tstage, ctstage, 3)
-        for copy in first:
-            copy.start()
         start(term_copies)
 
         for a in range(ROWS):
@@ -607,7 +613,7 @@
             pltpu.VMEM((16, 128, 128), bf16),
             pltpu.VMEM((4, 128, 128), bf16),
             pltpu.VMEM((162, 128, 256), f32),
-            pltpu.VMEM((ROWS, COLS, 8, 128), f32),
+            pltpu.VMEM((ROWS * 64, 128), f32),
             pltpu.VMEM((ROWS, COLS, 32, 128), f32),
             pltpu.VMEM((BLOCKS, 8, 32, 128), bf16),
             pltpu.VMEM((16 * FS, 128), f32),
@@ -621,7 +627,7 @@
             dma((2, n1)), dma((2, n1)), dma((2, n2)), dma((2, n2)),
         ],
         compiler_params=pltpu.CompilerParams(
-            collective_id=0, has_side_effects=True, vmem_limit_bytes=36 * 1024 * 1024
+            collective_id=0, has_side_effects=True, vmem_limit_bytes=60 * 1024 * 1024
         ),
     )(flat(position), flat(velocity), flat(other_accel), phase_ids, counts)
     new_pos, new_vel, pressure, monitor = pl.pallas_call(

time: 68.9 us -> 65.1 us (0.945)
  local copies, waits for them, and re-layouts: 3.72 us -> 0.89 us
    unnamed x10 -> x2, local copies, waits for them, and re-layouts: 3.72 us -> 0.89 us
where the time goes in v4:
time: 65.1 us; the launch traced here: 64.5 us
  Pallas kernels  62.9 us (97%)
  local copies, waits for them, and re-layouts  0.89 us (1%)
    pallas_call x1, Pallas kernels, local(): pl.pallas_call(kernel, out_shape=jax.ShapeDtypeStruct((OUT_ROWS, 128), f3...  62.3 us

profile of v4, /device:TPU:1, one launch (start us, length us, event | category | flops | bytes accessed | tf_op | source)
XLA Modules:
  0.0 64.5 jit_solution(6704080694364872099)
XLA Ops:
  0.6 62.3 %shard_map.84.in_ref = f32[200,128]{1,0:T(8,128)} custom-call(f32[72,128]{1,0:T(8,128)} %bitcast.15, f32[72,128]{1,0:T(8,128)} %bitcast.16, f32[72,128]{1,0:T(8,128)} %bitcast.17, s32[6,6,128]{2,1,0:T(8,128)} %phase_ref.1, s32[6,6]{1,0:T(8,128)} %counts_ref.1), custom_call_target="tpu_custom_call" | custom-call | tf_op jit(solution)/shard_map/pallas_call | solution.py:589
  62.9 0.0 copy-start
  62.9 0.9 %copy-done = f32[200,128]{1,0:T(8,128)S(1)} copy-done((f32[200,128]{1,0:T(8,128)S(1)}, f32[200,128]{1,0:T(8,128)}, u32[]{:S(2)}) %copy-start) | copy-done | bytes 102424
  63.8 0.6 shard_map.85
Async XLA Ops:
  62.9 0.9 %copy-start = (f32[200,128]{1,0:T(8,128)S(1)}, f32[200,128]{1,0:T(8,128)}, u32[]{:S(2)}) copy-start(f32[200,128]{1,0:T(8,128)} %shard_map.84.in_ref) | copy-start | bytes 307204

commit v5 on v4

--- a/solution.py
+++ b/solution.py
@@ -32,8 +32,13 @@
     (4, 5, 3, 4, 1), (4, 5, 4, 5, 1),
     (1, 4, 0, 5, 2),
 )
+ROW_TILES = (
+    (0, 1, 0, 1, 0), (0, 1, 1, 2, 0), (2, 2, 2, 3, 0),
+    (3, 4, 3, 4, 1), (3, 4, 4, 5, 1), (5, None, 5, None, 1),
+)
 GROUP_START = (0, 2)
-UNROLL = 8
+UNROLL_DENSITY = 5
+FORCE_FIRST = 4
 OUT_VELOCITY = ROWS * COLS * 2
 OUT_PRESSURE = 2 * OUT_VELOCITY
 OUT_MONITOR = OUT_PRESSURE + ROWS * 8
@@ -76,7 +81,7 @@
     pos_ref, vel_ref, oa_ref, phase_ref, counts_ref,
     out_ref,
     inp, inv, ino, inph, st, xp, bp, tp, stage, tstage, cstage, ctstage, rb, trb, crb, ctrb,
-    fb, ib, lt, gh, wb, da, fa, tf, mb, al, be, rl, ar0, ar1, ar2,
+    fb, ib, lt, gh, wb, aj, da, fa, tf, mb, al, be, rl, ar0, ar1, ar2,
     ins, hs, hr, ts, tr, a1s, a1r, a2s, a2r,
 ):
     index = {name: lax.axis_index(name) for name in SPLIT}
@@ -126,6 +131,7 @@
     xp[...] = jnp.full_like(xp, FAR)
     tp[...] = jnp.zeros_like(tp)
     fb[...] = jnp.zeros_like(fb)
+    aj[...] = jnp.zeros_like(aj)
     bp[...] = jnp.zeros_like(bp)
     rl[...] = jnp.zeros_like(rl)
     for buf in (stage, tstage, cstage, ctstage):
@@ -213,29 +219,37 @@
             pieces.append(jnp.zeros((32 * (blocks - 1 - block), 128), bf16))
         return jnp.concatenate(pieces, axis=0) if len(pieces) > 1 else part
 
-    def overlap(left, right, slot, sums, cols):
+    def collect(sums, col, part):
+        if col is not None:
+            sums[col] = part if sums[col] is None else sums[col] + part
+
+    def overlap(left, right, slot, sums, cols, mirrors=(None, None)):
         w = jnp.maximum(jnp.dot(left, right, preferred_element_type=f32), 0.0)
         w2 = w * w
         wb[slot] = w2
-        part = jnp.sum((w2 * w).reshape(16, 8, 256), axis=0)
+        w3 = w2 * w
+        part = jnp.sum(w3.reshape(16, 8, 256), axis=0)
         for e in range(2):
-            half = part[:, 128 * e : 128 * e + 128]
-            sums[cols[e]] = half if sums[cols[e]] is None else sums[cols[e]] + half
-
-    def own_tiles(a, ox3, lrow, slot, sums):
-        for q, (ca, cb, ja, jb, group) in enumerate(OWN_TILES):
-            pa = centre(a, ca, ox3 + (ja - ca + 1))
-            pb = centre(a, cb, ox3 + (jb - cb + 1))
-            if group == 2:
-                left = jnp.concatenate([lrow[0], lrow[1]], axis=1)
-                right = jnp.concatenate([at_block(pa, ja, 8), at_block(pb, jb - 2 + 4, 8)], axis=1)
-            else:
-                left = lrow[group]
-                right = jnp.concatenate(
-                    [at_block(pa, ja - GROUP_START[group], 4), at_block(pb, jb - GROUP_START[group], 4)],
-                    axis=1,
-                )
-            overlap(left, right, slot + q, sums, (ca, cb))
+            collect(sums, cols[e], part[:, 128 * e : 128 * e + 128])
+            if mirrors[e] is not None:
+                aj[mirrors[e]] += w3[:, 128 * e : 128 * e + 128]
+
+    def own_tiles(a, ox3, lrow, slot, sums, tiles=OWN_TILES, mirror_row=None):
+        for q, (ca, cb, ja, jb, group) in enumerate(tiles):
+            blocks = 8 if group == 2 else 4
+            halves = []
+            mirrors = []
+            for col, j, e in ((ca, ja, 0), (cb, jb, 1)):
+                if col is None:
+                    halves.append(jnp.zeros((32 * blocks, 128), bf16))
+                    mirrors.append(None)
+                    continue
+                block = (j + 2 * e if group == 2 else j - GROUP_START[group])
+                halves.append(at_block(centre(a, col, ox3 + (j - col + 1)), block, blocks))
+                keep = mirror_row is not None and not (tiles is ROW_TILES and col == j)
+                mirrors.append(mirror_row * COLS + j if keep else None)
+            left = jnp.concatenate([lrow[0], lrow[1]], axis=1) if group == 2 else lrow[group]
+            overlap(left, jnp.concatenate(halves, axis=1), slot + q, sums, (ca, cb), mirrors)
 
     def edge_tile(a, ox3, r, slot, sums):
         pa = centre(a, 0, ox3)
@@ -244,19 +258,33 @@
         right = jnp.concatenate([at_block(pa, 2 * odd, 4), at_block(pb, 2 * odd + 1, 4)], axis=1)
         overlap(gh[group], right, slot + 8, sums, (0, COLS - 1))
 
-    def pull(w2, left, sums, cols):
+    def halves_of(w2):
         hi = w2.astype(bf16)
-        lo = (w2 - hi.astype(f32)).astype(bf16)
+        return hi, (w2 - hi.astype(f32)).astype(bf16)
+
+    def pull(hi, lo, left, sums, cols):
         both = jnp.concatenate([left, left], axis=1)
         total = jnp.dot(both, jnp.concatenate([hi, lo], axis=0), preferred_element_type=f32)
         for e in range(2):
-            part = total[32 * e : 32 * e + 32, 128 * e : 128 * e + 128]
-            sums[cols[e]] = part if sums[cols[e]] is None else sums[cols[e]] + part
-
-    def own_pulls(r, slot, sums):
-        for q, (ca, cb, ja, jb, group) in enumerate(OWN_TILES):
-            left = jnp.concatenate([tf[r, ja], tf[r, jb]], axis=0)
-            pull(wb[slot + q], left, sums, (ca, cb))
+            collect(sums, cols[e], total[32 * e : 32 * e + 32, 128 * e : 128 * e + 128])
+
+    def pair_rows(block, ca, cb):
+        return jnp.concatenate([tf[block, ca], tf[block, ca if cb is None else cb]], axis=0)
+
+    def own_pulls(r, slot, sums, a=None, mirrored=None, tiles=OWN_TILES):
+        for q, (ca, cb, ja, jb, group) in enumerate(tiles):
+            hi, lo = halves_of(wb[slot + q])
+            pull(hi, lo, pair_rows(r, ja, jb), sums, (ca, cb))
+            if mirrored is None:
+                continue
+            row = tiles is ROW_TILES
+            cols = tuple(None if row and c == j else j for c, j in ((ca, ja), (cb, jb)))
+            if cols == (None, None):
+                continue
+            turn = [
+                jnp.concatenate([v[:, 0:128].T, v[:, 128:256].T], axis=1) for v in (hi, lo)
+            ]
+            pull(turn[0], turn[1], pair_rows(a, ca, cb), mirrored, cols)
 
     def side_cells(r):
         if r < 0:
@@ -329,19 +357,30 @@
         for r in range(ROWS):
             for g in range(2):
                 lt[(r + 1) * 2 + g] = turned([(r + 1) * 8 + GROUP_START[g] + s for s in range(4)])
-        da[...] = jnp.zeros_like(da)
-
-        def density(t, c):
-            a = t // 3
-            step = lax.rem(t, 3)
-            r = a + step
+        def row_with_itself(a, sums):
+            own_tiles(a, 3, (lt[(a + 1) * 2], lt[(a + 1) * 2 + 1]), (3 * a + 1) * 9, sums, ROW_TILES, a)
+            for s in range(COLS):
+                block = aj[a * COLS + s].T
+                aj[a * COLS + s] = jnp.zeros((128, 128), f32)
+                collect(sums, s, jnp.sum(block.reshape(16, 8, 128), axis=0))
+
+        def keep(a, sums):
+            for s in range(COLS):
+                da[pl.ds(a * 64 + s * 8, 8), :] = sums[s]
+
+        def density(a, c):
             sums = [None] * COLS
-            own_tiles(a, step * 3, (lt[r * 2], lt[r * 2 + 1]), t * 9, sums)
-            for s in range(COLS):
-                da[pl.ds(a * 64 + s * 8, 8), :] += sums[s]
+            row_with_itself(a, sums)
+            own_tiles(
+                a, 6, (lt[(a + 2) * 2], lt[(a + 2) * 2 + 1]), (3 * a + 2) * 9, sums, OWN_TILES, a + 1
+            )
+            keep(a, sums)
             return c
 
-        lax.fori_loop(1, 17, density, 0, unroll=UNROLL)
+        lax.fori_loop(0, ROWS - 1, density, 0, unroll=UNROLL_DENSITY)
+        sums = [None] * COLS
+        row_with_itself(ROWS - 1, sums)
+        keep(ROWS - 1, sums)
 
         diagonals, edges = position_copies
         for copy in edges:
@@ -441,19 +480,20 @@
         for a in range(ROWS):
             for s in range(COLS):
                 tf[a + 1, s] = cell(fb, (a + 1) * 8 + s).astype(bf16)
-        fa[...] = jnp.zeros_like(fa)
-
-        def force(t, c):
-            a = t // 3
-            step = lax.rem(t, 3)
-            sums = [None] * COLS
-            own_pulls(a + step, t * 9, sums)
+
+        def force(a, c):
+            here = [None] * COLS
+            below = [None] * COLS
+            own_pulls(a + 1, (3 * a + 1) * 9, here, a + 1, here, ROW_TILES)
+            own_pulls(a + 2, (3 * a + 2) * 9, here, a + 1, below, OWN_TILES)
             for s in range(COLS):
-                fa[a, s] += sums[s]
+                fa[a, s] += here[s]
+                fa[a + 1, s] = below[s]
             return c
 
-        lax.fori_loop(1, 17, force, 0, unroll=UNROLL)
-
+        for s in range(COLS):
+            fa[0, s] = jnp.zeros((32, 128), f32)
+        lax.fori_loop(0, FORCE_FIRST, force, 0)
         for copy in first:
             copy.wait()
         best = vec
@@ -463,6 +503,11 @@
         second = bounds_copies(now, 1, ar2, a2s, a2r, second_peers)
         for copy in second:
             copy.start()
+
+        lax.fori_loop(FORCE_FIRST, ROWS - 1, force, 0)
+        here = [None] * COLS
+        own_pulls(ROWS, (3 * ROWS - 2) * 9, here, ROWS, here, ROW_TILES)
+        add_up(fa, ROWS - 1, here)
 
         diagonals, edges = term_copies
         for copy in edges:
@@ -480,7 +525,8 @@
 
         def side_pull(t, r, sums):
             (lb, ls), (ub, us) = side_cells(r)
-            pull(wb[t * 9 + 8], jnp.concatenate([tf[lb, ls], tf[ub, us]], axis=0), sums, (0, COLS - 1))
+            hi, lo = halves_of(wb[t * 9 + 8])
+            pull(hi, lo, jnp.concatenate([tf[lb, ls], tf[ub, us]], axis=0), sums, (0, COLS - 1))
 
         for t, a, ox, r, row in side_tiles("edges"):
             sums = [None] * COLS
@@ -613,6 +659,7 @@
             pltpu.VMEM((16, 128, 128), bf16),
             pltpu.VMEM((4, 128, 128), bf16),
             pltpu.VMEM((162, 128, 256), f32),
+            pltpu.VMEM((ROWS * COLS, 128, 128), f32),
             pltpu.VMEM((ROWS * 64, 128), f32),
             pltpu.VMEM((ROWS, COLS, 32, 128), f32),
             pltpu.VMEM((BLOCKS, 8, 32, 128), bf16),

time: 65.1 us -> 62.8 us (0.965)
  Pallas kernels: 62.9 us -> 61 us
    pallas_call x1, Pallas kernels: 62.3 us -> 60.4 us  [local(): pl.pallas_call(kernel, out_shape=jax.ShapeDtypeStruct((OUT_ROWS, 128), f3...]
where the time goes in v5:
time: 62.8 us; the launch traced here: 62.6 us
  Pallas kernels  61 us (97%)
  local copies, waits for them, and re-layouts  0.89 us (1%)
  between operations  0.65 us (1%)
    pallas_call x1, Pallas kernels, local(): pl.pallas_call(kernel, out_shape=jax.ShapeDtypeStruct((OUT_ROWS, 128), f3...  60.4 us

profile of v5, /device:TPU:1, one launch (start us, length us, event | category | flops | bytes accessed | tf_op | source)
XLA Modules:
  0.0 62.6 jit_solution(8446964106958022004)
XLA Ops:
  0.6 60.4 %shard_map.84.in_ref = f32[200,128]{1,0:T(8,128)} custom-call(f32[72,128]{1,0:T(8,128)} %bitcast.15, f32[72,128]{1,0:T(8,128)} %bitcast.16, f32[72,128]{1,0:T(8,128)} %bitcast.17, s32[6,6,128]{2,1,0:T(8,128)} %phase_ref.1, s32[6,6]{1,0:T(8,128)} %counts_ref.1), custom_call_target="tpu_custom_call" | custom-call | tf_op jit(solution)/shard_map/pallas_call | solution.py:635
  61.0 0.0 copy-start
  61.0 0.9 %copy-done = f32[200,128]{1,0:T(8,128)S(1)} copy-done((f32[200,128]{1,0:T(8,128)S(1)}, f32[200,128]{1,0:T(8,128)}, u32[]{:S(2)}) %copy-start) | copy-done | bytes 102424
  61.9 0.6 %shard_map.85 = (f32[72,128]{1,0:T(8,128)}, f32[72,128]{1,0:T(8,128)}, f32[6,6,128]{2,1,0:T(8,128)}, f32[4,4]{1,0:T(4,128)}) custom-call(f32[200,128]{1,0:T(8,128)S(1)} %copy-done), custom_call_target="tpu_custom_call" | custom-call | tf_op jit(solution)/shard_map/pallas_call | solution.py:680
Async XLA Ops:
  61.0 0.9 %copy-start = (f32[200,128]{1,0:T(8,128)S(1)}, f32[200,128]{1,0:T(8,128)}, u32[]{:S(2)}) copy-start(f32[200,128]{1,0:T(8,128)} %shard_map.84.in_ref) | copy-start | bytes 307204

commit v6 on v5

--- a/solution.py
+++ b/solution.py
@@ -39,6 +39,7 @@
 GROUP_START = (0, 2)
 UNROLL_DENSITY = 5
 FORCE_FIRST = 4
+EDGE_FIRST = 9
 OUT_VELOCITY = ROWS * COLS * 2
 OUT_PRESSURE = 2 * OUT_VELOCITY
 OUT_MONITOR = OUT_PRESSURE + ROWS * 8
@@ -308,8 +309,6 @@
                 rows[28 + q] = rnd(field - rows[24 + q])
         return rows
 
-    pl.semaphore_wait(barrier, len(neighbours) + len(first_peers) + len(second_peers))
-
     position_copies = halo_copies(bp, stage, cstage, rb, crb, hs, hr)
     term_copies = halo_copies(tp, tstage, ctstage, trb, ctrb, ts, tr)
 
@@ -326,7 +325,6 @@
             bp[3 * f + 1, 1 : ROWS + 1] = step * st[8 + 3 * f]
             bp[3 * f + 2, 1 : ROWS + 1] = step * st[9 + 3 * f]
         pack(bp, stage, cstage, 6)
-        start(position_copies)
 
     def side_tiles(which):
         done = []
@@ -378,10 +376,6 @@
             return c
 
         lax.fori_loop(0, ROWS - 1, density, 0, unroll=UNROLL_DENSITY)
-        sums = [None] * COLS
-        row_with_itself(ROWS - 1, sums)
-        keep(ROWS - 1, sums)
-
         diagonals, edges = position_copies
         for copy in edges:
             copy.wait()
@@ -396,16 +390,23 @@
                 lt[block * 2 + g] = turned([block * 8 + GROUP_START[g] + s for s in range(4)])
         for q in range(3):
             gh[q] = turned([b * 8 + s for r in (2 * q, 2 * q + 1) for b, s in side_cells(r)])
-        for t, a, ox, r, row in side_tiles("edges"):
-            sums = [None] * COLS
-            if row:
-                own_tiles(a, (ox + 1) * 3, (lt[(r + 1) * 2], lt[(r + 1) * 2 + 1]), t * 9, sums)
-            else:
-                edge_tile(a, (ox + 1) * 3, r, t * 9, sums)
-            for s in range(COLS):
-                if sums[s] is not None:
-                    da[a * 64 + s * 8 : a * 64 + s * 8 + 8, :] += sums[s]
-
+        sums = [None] * COLS
+        row_with_itself(ROWS - 1, sums)
+        keep(ROWS - 1, sums)
+
+        def side_density(tiles):
+            for t, a, ox, r, row in tiles:
+                sums = [None] * COLS
+                if row:
+                    own_tiles(a, (ox + 1) * 3, (lt[(r + 1) * 2], lt[(r + 1) * 2 + 1]), t * 9, sums)
+                else:
+                    edge_tile(a, (ox + 1) * 3, r, t * 9, sums)
+                for s in range(COLS):
+                    if sums[s] is not None:
+                        da[a * 64 + s * 8 : a * 64 + s * 8 + 8, :] += sums[s]
+
+        edge_tiles = side_tiles("edges")
+        side_density(edge_tiles[:EDGE_FIRST])
         for copy in diagonals:
             copy.wait()
         for d in range(4):
@@ -417,12 +418,7 @@
         jrow, _ = feature_rows(xp[0, CORNERS], xp[1, CORNERS])
         put(fb, jrow, CORNERS * 8)
         gh[3] = turned([CORNERS * 8 + q for q in range(4)])
-        for t, a, ox, r, row in side_tiles("corners"):
-            sums = [None] * COLS
-            edge_tile(a, (ox + 1) * 3, r, t * 9, sums)
-            for s in range(COLS):
-                if sums[s] is not None:
-                    da[a * 64 + s * 8 : a * 64 + s * 8 + 8, :] += sums[s]
+        side_density(edge_tiles[EDGE_FIRST:-1] + side_tiles("corners") + edge_tiles[-1:])
 
     def bounds_copies(now, src_slot, dst, send, recv, targets):
         return [
@@ -576,6 +572,7 @@
         @pl.when(it < ITERS - 1)
         def _():
             coefficients()
+            start(position_copies)
 
         for copy in second:
             copy.wait()
@@ -591,6 +588,8 @@
             st[6, a] = jnp.where(alive[a], st[6, a] + relax * excess[a], 0.0)
 
     coefficients()
+    pl.semaphore_wait(barrier, len(neighbours) + len(first_peers) + len(second_peers))
+    start(position_copies)
 
     def whole(it, carry):
         densities(it)
@@ -610,12 +609,18 @@
         out_ref[OUT_PRESSURE + a * 8 : OUT_PRESSURE + a * 8 + 8, :] = st[6, a]
 
 
-def spread(in_ref, npos_ref, nvel_ref, pres_ref, mon_ref):
-    npos_ref[...] = in_ref[0:OUT_VELOCITY, :]
-    nvel_ref[...] = in_ref[OUT_VELOCITY:OUT_PRESSURE, :]
+def spread(in_ref, npos_ref, nvel_ref, pres_ref, mon_ref, rest, sems):
+    copies = [
+        pltpu.make_async_copy(in_ref.at[pl.ds(first, out.shape[0])], out, sems.at[q])
+        for q, (first, out) in enumerate(((0, npos_ref), (OUT_VELOCITY, nvel_ref), (OUT_PRESSURE, rest)))
+    ]
+    for copy in copies:
+        copy.start()
+    for copy in copies:
+        copy.wait()
     for a in range(ROWS):
-        pres_ref[a] = in_ref[OUT_PRESSURE + a * 8 : OUT_PRESSURE + a * 8 + COLS, :]
-    mon_ref[...] = in_ref[OUT_MONITOR : OUT_MONITOR + ITERS, 0:4]
+        pres_ref[a] = rest[a * 8 : a * 8 + COLS, :]
+    mon_ref[...] = rest[ROWS * 8 : ROWS * 8 + ITERS, 0:4]
 
 
 def flat(value):
@@ -685,9 +690,10 @@
             jax.ShapeDtypeStruct((ROWS, COLS, 128), f32),
             jax.ShapeDtypeStruct((ITERS, 4), f32),
         ),
-        in_specs=[vmem],
+        in_specs=[hbm],
         out_specs=[vmem] * 4,
-        compiler_params=pltpu.CompilerParams(vmem_limit_bytes=4 * 1024 * 1024),
+        scratch_shapes=[pltpu.VMEM((OUT_ROWS - OUT_PRESSURE, 128), f32), dma((3,))],
+        compiler_params=pltpu.CompilerParams(vmem_limit_bytes=60 * 1024 * 1024),
     )(packed)
     return unflat(new_pos), unflat(new_vel), pressure, monitor
 

time: 62.8 us -> 61.7 us (0.982)
  local copies, waits for them, and re-layouts: 0.89 us -> 0 us
    pallas_call x1, Pallas kernels: 60.4 us -> 59.3 us  [local(): pl.pallas_call(kernel, out_shape=jax.ShapeDtypeStruct((OUT_ROWS, 128), f3...]
    unnamed x2 -> x0, local copies, waits for them, and re-layouts: 0.89 us -> none
    pallas_call x1, Pallas kernels: 0.64 us -> 1.45 us  [local(): pl.pallas_call(spread, out_shape=(jax.ShapeDtypeStruct((ROWS * COLS * 2,...]
where the time goes in v6:
time: 61.7 us; the launch traced here: 61.4 us
  Pallas kernels  60.8 us (99%)
  between operations  0.64 us (1%)
    pallas_call x1, Pallas kernels, local(): pl.pallas_call(kernel, out_shape=jax.ShapeDtypeStruct((OUT_ROWS, 128), f3...  59.3 us
    pallas_call x1, Pallas kernels, local(): pl.pallas_call(spread, out_shape=(jax.ShapeDtypeStruct((ROWS * COLS * 2,...  1.45 us

profile of v6, /device:TPU:1, one launch (start us, length us, event | category | flops | bytes accessed | tf_op | source)
XLA Modules:
  0.0 61.4 jit_solution(7808129461869079207)
XLA Ops:
  0.6 59.3 %shard_map.84.in_ref = f32[200,128]{1,0:T(8,128)} custom-call(f32[72,128]{1,0:T(8,128)} %bitcast.15, f32[72,128]{1,0:T(8,128)} %bitcast.16, f32[72,128]{1,0:T(8,128)} %bitcast.17, s32[6,6,128]{2,1,0:T(8,128)} %phase_ref.1, s32[6,6]{1,0:T(8,128)} %counts_ref.1), custom_call_target="tpu_custom_call" | custom-call | tf_op jit(solution)/shard_map/pallas_call | solution.py:640
  60.0 1.4 %shard_map.85 = (f32[72,128]{1,0:T(8,128)}, f32[72,128]{1,0:T(8,128)}, f32[6,6,128]{2,1,0:T(8,128)}, f32[4,4]{1,0:T(4,128)}) custom-call(f32[200,128]{1,0:T(8,128)} %shard_map.84.in_ref), custom_call_target="tpu_custom_call" | custom-call | tf_op jit(solution)/shard_map/pallas_call | solution.py:685

commit v7 on v6

--- a/solution.py
+++ b/solution.py
@@ -39,7 +39,7 @@
 GROUP_START = (0, 2)
 UNROLL_DENSITY = 5
 FORCE_FIRST = 4
-EDGE_FIRST = 9
+EDGE_FIRST = 5
 OUT_VELOCITY = ROWS * COLS * 2
 OUT_PRESSURE = 2 * OUT_VELOCITY
 OUT_MONITOR = OUT_PRESSURE + ROWS * 8

time: 61.7 us -> 61.7 us (level)
  no operation moved by 1% of the time
where the time goes in v7:
time: 61.7 us; the launch traced here: 61.4 us
  Pallas kernels  60.8 us (99%)
  between operations  0.64 us (1%)
    pallas_call x1, Pallas kernels, local(): pl.pallas_call(kernel, out_shape=jax.ShapeDtypeStruct((OUT_ROWS, 128), f3...  59.4 us
    pallas_call x1, Pallas kernels, local(): pl.pallas_call(spread, out_shape=(jax.ShapeDtypeStruct((ROWS * COLS * 2,...  1.45 us

profile of v7, /device:TPU:1, one launch (start us, length us, event | category | flops | bytes accessed | tf_op | source)
XLA Modules:
  0.0 61.4 jit_solution(7146797177702966342)
XLA Ops:
  0.6 59.4 %shard_map.84.in_ref = f32[200,128]{1,0:T(8,128)} custom-call(f32[72,128]{1,0:T(8,128)} %bitcast.15, f32[72,128]{1,0:T(8,128)} %bitcast.16, f32[72,128]{1,0:T(8,128)} %bitcast.17, s32[6,6,128]{2,1,0:T(8,128)} %phase_ref.1, s32[6,6]{1,0:T(8,128)} %counts_ref.1), custom_call_target="tpu_custom_call" | custom-call | tf_op jit(solution)/shard_map/pallas_call | solution.py:640
  60.0 1.4 %shard_map.85 = (f32[72,128]{1,0:T(8,128)}, f32[72,128]{1,0:T(8,128)}, f32[6,6,128]{2,1,0:T(8,128)}, f32[4,4]{1,0:T(4,128)}) custom-call(f32[200,128]{1,0:T(8,128)} %shard_map.84.in_ref), custom_call_target="tpu_custom_call" | custom-call | tf_op jit(solution)/shard_map/pallas_call | solution.py:685
